TPU v7x, 32 devices: a whole 2x2x4 slice. The times are simulated.
32 devices in a mesh: dp: 4 (over z), rows: 8 (over y, x, core).
Axes of the slice: x: 2, y: 2, z: 4, core: 2. Of those that a mesh axis runs over, the one named last changes fastest.
Arguments:
- latent: bfloat16 [8, 8, 64, 640], P('dp', 'rows'), may hold values from -16.25 to 16.25
- hidden: bfloat16 [8, 8, 64, 640], P('dp', 'rows'), may hold values from -16.25 to 16.25
- cotangent: bfloat16 [8, 8, 64, 640], P('dp', 'rows'), may hold values from -6 to 6
- filter_one: bfloat16 [9, 640, 640], P(None, 'dp', 'rows'), may hold values from -0.078125 to 0.078125
- filter_two: bfloat16 [9, 640, 640], P(None, 'dp', 'rows'), may hold values from -0.078125 to 0.078125
- gain_one: float32 [640], replicated, may hold values from 0.1 to 1.9
- shift_one: float32 [640], replicated, may hold values from -2.5 to 2.5
- gain_two: float32 [640], replicated, may hold values from 0.1 to 1.9
- shift_two: float32 [640], replicated, may hold values from -2.5 to 2.5
Outputs:
- latent_grad: bfloat16 [8, 8, 64, 640], P('dp', 'rows')
All inputs are finite; a program needn't handle non-finite values.
Results may differ from a plain program's by a relative error of at most 0.0027.
Values may be sent and summed in bfloat16 or wider, within the bound.
No kernel may reach another device: no remote copies, remote signals or barrier semaphores. Data moves between devices by JAX's collectives and lax.ppermute only.
A program may use at most 128 MiB of HBM per device.

v0:
```python
import jax
import jax.numpy as jnp
from jax import lax
from jax.sharding import PartitionSpec as P

GROUPS = 16
GSIZE = 40


def extended(block, sides, width):
    for axis, dim in sides:
        count = lax.axis_size(axis)
        forward = [(i, i + 1) for i in range(count - 1)]
        backward = [(target, source) for source, target in forward]
        low = lax.ppermute(
            lax.slice_in_dim(block, block.shape[dim] - width, None, axis=dim), axis, forward
        )
        high = lax.ppermute(lax.slice_in_dim(block, 0, width, axis=dim), axis, backward)
        block = jnp.concatenate([low, block, high], axis=dim)
    return block


def group_sums(values):
    per_channel = jnp.sum(values, axis=(1, 2))
    return jnp.sum(per_channel.reshape(per_channel.shape[0], GROUPS, -1), axis=2)


def expand_groups(moment):
    return jnp.repeat(moment, GSIZE, axis=1)[:, None, None, :]


def finish_stats(sum_plain, sum_square, number):
    average = sum_plain / number
    variance = sum_square / number - average * average
    return (average, lax.rsqrt(variance + 1e-05))


def reduced_stats(field, number):
    values = field.astype(jnp.float32)
    sum_plain, sum_square = lax.psum((group_sums(values), group_sums(values * values)), "rows")
    return finish_stats(sum_plain, sum_square, number)


def norm_backward(field, stats, gain, shift, incoming, number):
    average, inverse = stats
    values = field.astype(jnp.float32)
    normed = (values - expand_groups(average)) * expand_groups(inverse)
    linear = normed * gain + shift
    logistic = jax.nn.sigmoid(linear)
    scaled = incoming * logistic * (1.0 + linear * (1.0 - logistic)) * gain
    sum_first, sum_second = lax.psum((group_sums(scaled), group_sums(scaled * normed)), "rows")
    first = sum_first / number
    second = sum_second / number
    return expand_groups(inverse) * (scaled - expand_groups(first) - normed * expand_groups(second))


def conv_backward(gradient, weights):
    images, rows_here, breadth, channels = gradient.shape
    padded = extended(gradient, (("rows", 1),), 1)
    padded = jnp.pad(padded, ((0, 0), (0, 0), (1, 1), (0, 0)))
    pixels = images * rows_here * breadth
    shifted = []
    for tap_index in range(9):
        down_step = tap_index // 3 - 1
        side_step = tap_index % 3 - 1
        window = padded[
            :, 1 - down_step : 1 - down_step + rows_here, 1 - side_step : 1 - side_step + breadth, :
        ]
        shifted.append(window.reshape(pixels, channels))
    stacked = jnp.stack(shifted, axis=1)
    gathered = lax.all_gather(weights, "dp", axis=1, tiled=True)
    section = lax.all_gather(gathered, "rows", axis=2, tiled=True)
    columns = section.shape[2]
    window = stacked.reshape(pixels, 9 * columns)
    flat = jnp.transpose(section, (0, 2, 1)).reshape(9 * columns, section.shape[1])
    result = jnp.dot(window, flat, preferred_element_type=jnp.float32)
    return result.reshape(images, rows_here, breadth, channels)


def body(
    latent, hidden, cotangent, filter_one, filter_two, gain_one, shift_one, gain_two, shift_two
):
    number = latent.shape[1] * lax.axis_size("rows") * latent.shape[2] * GSIZE
    stats_two = reduced_stats(hidden, number)
    back_two = conv_backward(cotangent, filter_two)
    hidden_grad = norm_backward(hidden, stats_two, gain_two, shift_two, back_two, number).astype(
        jnp.bfloat16
    )
    stats_one = reduced_stats(latent, number)
    back_one = conv_backward(hidden_grad, filter_one)
    latent_part = norm_backward(latent, stats_one, gain_one, shift_one, back_one, number)
    return (cotangent.astype(jnp.float32) + latent_part).astype(jnp.bfloat16)


def solution(mesh):
    in_specs = (
        P("dp", "rows", None, None),
        P("dp", "rows", None, None),
        P("dp", "rows", None, None),
        P(None, "dp", "rows"),
        P(None, "dp", "rows"),
        P(),
        P(),
        P(),
        P(),
    )
    out_specs = P("dp", "rows", None, None)
    return jax.shard_map(body, mesh=mesh, in_specs=in_specs, out_specs=out_specs, check_vma=False)
```

profile of v0, /device:TPU:28, one launch (start us, length us, event | category | flops | bytes accessed | tf_op | source)
XLA Modules:
  0.0 223.1 jit_solution(1200964164859489196)
XLA Ops:
  6.5 1.2 copy.112
  7.7 47.0 %all_gather.12 = bf16[9,640,80]{2,0,1:T(8,128)(2,1)S(1)} all-gather(bf16[9,160,80]{2,0,1:T(8,128)(2,1)S(1)} %copy.112), channel_id=1, replica_groups=mesh['dp'=4,'rows'=8] {'dp'}, dimensions={1}, use_global_device_ids=true | all-gather | bytes 1152000 | tf_op jit(solution)/shard_map/all_gather | solution.py:71
  54.7 3.0 %copy.113 = bf16[9,640,80]{1,2,0:T(8,128)(2,1)} copy(bf16[9,640,80]{2,0,1:T(8,128)(2,1)S(1)} %all_gather.12) | data formatting | bytes 1843200 | tf_op jit(solution)/shard_map/all_gather | solution.py:71
  58.0 45.9 %all_gather.14 = bf16[9,640,80]{2,0,1:T(8,128)(2,1)S(1)} all-gather(bf16[9,160,80]{2,0,1:T(8,128)(2,1)S(1)} %copy.123), channel_id=1, replica_groups=mesh['dp'=4,'rows'=8] {'dp'}, dimensions={1}, use_global_device_ids=true | all-gather | bytes 1152000 | tf_op jit(solution)/shard_map/all_gather | solution.py:71
  103.8 3.0 %copy.124 = bf16[9,640,80]{1,2,0:T(8,128)(2,1)} copy(bf16[9,640,80]{2,0,1:T(8,128)(2,1)S(1)} %all_gather.14) | data formatting | bytes 1843200 | tf_op jit(solution)/shard_map/all_gather | solution.py:71
  106.9 2.1 collective-permute-start
  108.9 4.5 %collective-permute-start.1 = (bf16[2,1,64,640]{3,2,1,0:T(8,128)(2,1)S(1)}, bf16[2,1,64,640]{3,2,1,0:T(8,128)(2,1)S(1)}, u32[]{:S(2)}, u32[]{:S(2)}) collective-permute-start(bf16[2,1,64,640]{3,2,1,0:T(8,128)(2,1)S(1)} %copy-done), channel_id=1, source_target_pairs={{1,0},{2,1},{3,2},{4,3},{5,4},{6,5},{7,6},{9,8},{10,9},{11,10},{12... | collective-permute-start | bytes 491528 | tf_op jit(solution)/shard_map/ppermute | solution.py:18
  113.9 12.3 %all-reduce.4 = (f32[2,16]{1,0:T(2,128)S(1)}, f32[2,16]{1,0:T(2,128)S(1)}) all-reduce(f32[2,16]{1,0:T(2,128)S(1)} %reduce_sum.151, f32[2,16]{1,0:T(2,128)S(1)} %reduce_sum.149), channel_id=1, replica_groups=mesh['dp'=4,'rows'=8] {'rows'}, use_global_device_ids=true, to_apply=%region_11.12 | all-reduce | flops 64 | bytes 512 | tf_op jit(solution)/shard_map/psum | solution.py:40
  127.9 1.0 copy.105
  129.8 1.0 copy.108
  130.8 1.0 copy.109
  131.8 1.0 copy.111
  132.8 1.0 copy.104
  133.8 1.0 copy.110
  134.8 11.1 %stack.6 = bf16[128,9,640]{2,1,0:T(8,128)(2,1)S(1)} concatenate(bf16[128,1,640]{2,1,0:T(2,128)(2,1)S(1)} %copy.103, bf16[128,1,640]{2,1,0:T(2,128)(2,1)} %copy.104, bf16[128,1,640]{2,1,0:T(2,128)(2,1)} %copy.105, bf16[128,1,640]{2,1,0:T(2,128)(2,1)} %copy.106, bf16[128,1,640]{2,1,0:T(2,128)(2,1)S(1)} %copy.107, bf16[128,1,640]{2,1,0:T(2,128)(2,1)} %copy.108, ...), dimensions={1} | concatenate | bytes 2949120 | tf_op jit(solution)/shard_map/stack | solution.py:70
  145.9 1.8 reshape.88
  147.7 5.1 %fusion.53 = (f32[2,640]{1,0:T(2,128)S(1)}, f32[2,640]{1,0:T(2,128)S(1)}, f32[2,1,64,640]{3,2,0,1:T(8,128)S(1)}) fusion(f32[2,640]{1,0:T(2,128)S(1)} %mul.122, f32[2,640]{1,0:T(2,128)S(1)} %sub.60, bf16[2,1,64,640]{3,2,1,0:T(8,128)(2,1)S(1)} %copy-done.4, f32[640]{0:T(1024)S(1)} %copy-done.6, f32[640]{0:T(1024)S(1)} %copy-done.7, ...), kind=kOutput, calls=%fused_computation.73 | convolution fusion | flops 945108480 | bytes 9364480 | tf_op jit(solution)/shard_map/dot_general | solution.py:76
  153.1 12.0 %all-reduce.3 = (f32[2,16]{1,0:T(2,128)S(1)}, f32[2,16]{1,0:T(2,128)S(1)}, f32[2,16]{1,0:T(2,128)S(1)}, f32[2,16]{1,0:T(2,128)S(1)}) all-reduce(f32[2,16]{1,0:T(2,128)S(1)} %reduce_sum.155, f32[2,16]{1,0:T(2,128)S(1)} %reduce_sum.153, f32[2,16]{1,0:T(2,128)S(1)} %reduce_sum.147, ...), channel_id=1, replica_groups=mesh['dp'=4,'rows'=8] {'rows'}, use_global_device_ids=true, to_apply=%region_17.18 | all-reduce | flops 128 | bytes 1024 | tf_op jit(solution)/shard_map/psum | solution.py:51
  165.5 1.9 collective-permute-start.2
  167.5 4.7 %collective-permute-start.3 = (bf16[2,1,64,640]{3,2,0,1:T(8,128)(2,1)S(1)}, bf16[2,1,64,640]{3,2,0,1:T(8,128)(2,1)S(1)}, u32[]{:S(2)}, u32[]{:S(2)}) collective-permute-start(bf16[2,1,64,640]{3,2,0,1:T(8,128)(2,1)S(1)} %fusion.50), channel_id=1, source_target_pairs={{1,0},{2,1},{3,2},{4,3},{5,4},{6,5},{7,6},{9,8},{10,9},{11,10},{12... | collective-permute-start | bytes 491528 | tf_op jit(solution)/shard_map/ppermute | solution.py:18
  172.8 1.2 collective-permute-done.2
  175.4 1.0 copy.116
  176.4 1.0 copy.117
  177.4 1.0 copy.119
  178.4 1.0 copy.120
  179.4 1.0 copy.122
  180.3 1.0 copy.115
  181.3 1.0 copy.121
  182.3 11.0 %stack.7 = bf16[128,9,640]{2,1,0:T(8,128)(2,1)S(1)} concatenate(bf16[128,1,640]{2,1,0:T(2,128)(2,1)S(1)} %copy.114, bf16[128,1,640]{2,1,0:T(2,128)(2,1)} %copy.115, bf16[128,1,640]{2,1,0:T(2,128)(2,1)} %copy.116, bf16[128,1,640]{2,1,0:T(2,128)(2,1)} %copy.117, bf16[128,1,640]{2,1,0:T(2,128)(2,1)S(1)} %copy.118, bf16[128,1,640]{2,1,0:T(2,128)(2,1)} %copy.119, ...), dimensions={1} | concatenate | bytes 2949120 | tf_op jit(solution)/shard_map/stack | solution.py:70
  193.4 1.8 reshape.92
  195.2 4.9 %fusion.52 = (f32[2,640]{1,0:T(2,128)S(1)}, f32[2,640]{1,0:T(2,128)S(1)}, f32[2,1,64,640]{3,2,0,1:T(8,128)S(1)}) fusion(f32[2,640]{1,0:T(2,128)S(1)} %mul.118, f32[2,640]{1,0:T(2,128)S(1)} %sub.68, bf16[2,1,64,640]{3,2,1,0:T(8,128)(2,1)S(1)} %copy-done.2, f32[640]{0:T(1024)S(1)} %copy-done.8, f32[640]{0:T(1024)S(1)} %copy-done.9, ...), kind=kOutput, calls=%fused_computation.72 | convolution fusion | flops 945108480 | bytes 9364480 | tf_op jit(solution)/shard_map/dot_general | solution.py:76
  200.5 14.6 %all-reduce.2 = (f32[2,16]{1,0:T(2,128)S(1)}, f32[2,16]{1,0:T(2,128)S(1)}) all-reduce(f32[2,16]{1,0:T(2,128)S(1)} %reduce_sum.159, f32[2,16]{1,0:T(2,128)S(1)} %reduce_sum.157), channel_id=1, replica_groups=mesh['dp'=4,'rows'=8] {'rows'}, use_global_device_ids=true, to_apply=%region_23.24 | all-reduce | flops 64 | bytes 512 | tf_op jit(solution)/shard_map/psum | solution.py:51
  (80 shorter events, 7.5 us)
Async XLA Ops:
  6.5 141.2 %all-gather.3.cloned.1.call-start = ((), (), s32[]{:S(2)}) async-start(), calls=%async_computation | async-start | bytes 8294400 | tf_op jit(solution)/shard_map/all_gather | solution.py:72
  54.7 3.1 %copy-start.5 = (bf16[9,160,80]{2,1,0:T(8,128)(2,1)S(1)}, bf16[9,160,80]{2,1,0:T(8,128)(2,1)}, u32[]{:S(2)}) copy-start(bf16[9,160,80]{2,1,0:T(8,128)(2,1)} %param.12) | copy-start | bytes 691204
  57.7 137.5 %all-gather.5.cloned.1.call-start = ((), (), s32[]{:S(2)}) async-start(), calls=%async_computation.1 | async-start | bytes 8294400 | tf_op jit(solution)/shard_map/all_gather | solution.py:72
  103.8 3.0 %copy-start = (bf16[2,1,64,640]{3,2,1,0:T(8,128)(2,1)S(1)}, bf16[2,1,64,640]{3,2,1,0:T(8,128)(2,1)}, u32[]{:S(2)}) copy-start(bf16[2,1,64,640]{3,2,1,0:T(8,128)(2,1)} %param.11) | copy-start | bytes 491524
  103.8 9.6 %copy-start.3 = (bf16[2,1,64,640]{3,2,1,0:T(8,128)(2,1)S(1)}, bf16[2,1,64,640]{3,2,1,0:T(8,128)(2,1)}, u32[]{:S(2)}) copy-start(bf16[2,1,64,640]{3,2,1,0:T(8,128)(2,1)} %param.10) | copy-start | bytes 491524
  106.8 20.0 %copy-start.1 = (bf16[2,1,64,640]{3,2,1,0:T(8,128)(2,1)S(1)}, bf16[2,1,64,640]{3,2,1,0:T(8,128)(2,1)}, u32[]{:S(2)}) copy-start(bf16[2,1,64,640]{3,2,1,0:T(8,128)(2,1)} %param.9) | copy-start | bytes 491524
  106.9 20.4 %collective-permute-start = (bf16[2,1,64,640]{3,2,1,0:T(8,128)(2,1)S(1)}, bf16[2,1,64,640]{3,2,1,0:T(8,128)(2,1)S(1)}, u32[]{:S(2)}, u32[]{:S(2)}) collective-permute-start(bf16[2,1,64,640]{3,2,1,0:T(8,128)(2,1)S(1)} %copy-done), channel_id=1, source_target_pairs={{0,1},{1,2},{2,3},{3,4},{4,5},{5,6},{6,7},{8,9},{9,10},{10,11},{11... | collective-permute-start | bytes 491528 | tf_op jit(solution)/shard_map/ppermute | solution.py:15
  108.9 18.4 %collective-permute-start.1 = (bf16[2,1,64,640]{3,2,1,0:T(8,128)(2,1)S(1)}, bf16[2,1,64,640]{3,2,1,0:T(8,128)(2,1)S(1)}, u32[]{:S(2)}, u32[]{:S(2)}) collective-permute-start(bf16[2,1,64,640]{3,2,1,0:T(8,128)(2,1)S(1)} %copy-done), channel_id=1, source_target_pairs={{1,0},{2,1},{3,2},{4,3},{5,4},{6,5},{7,6},{9,8},{10,9},{11,10},{12... | collective-permute-start | bytes 491528 | tf_op jit(solution)/shard_map/ppermute | solution.py:18
  145.9 1.8 copy-start.4
  145.9 1.8 copy-start.6
  145.9 1.8 copy-start.7
  165.5 8.4 %collective-permute-start.2 = (bf16[2,1,64,640]{3,2,0,1:T(8,128)(2,1)S(1)}, bf16[2,1,64,640]{3,2,0,1:T(8,128)(2,1)S(1)}, u32[]{:S(2)}, u32[]{:S(2)}) collective-permute-start(bf16[2,1,64,640]{3,2,0,1:T(8,128)(2,1)S(1)} %fusion.50), channel_id=1, source_target_pairs={{0,1},{1,2},{2,3},{3,4},{4,5},{5,6},{6,7},{8,9},{9,10},{10,11},{11... | collective-permute-start | bytes 491528 | tf_op jit(solution)/shard_map/ppermute | solution.py:15
  167.5 7.4 %collective-permute-start.3 = (bf16[2,1,64,640]{3,2,0,1:T(8,128)(2,1)S(1)}, bf16[2,1,64,640]{3,2,0,1:T(8,128)(2,1)S(1)}, u32[]{:S(2)}, u32[]{:S(2)}) collective-permute-start(bf16[2,1,64,640]{3,2,0,1:T(8,128)(2,1)S(1)} %fusion.50), channel_id=1, source_target_pairs={{1,0},{2,1},{3,2},{4,3},{5,4},{6,5},{7,6},{9,8},{10,9},{11,10},{12... | collective-permute-start | bytes 491528 | tf_op jit(solution)/shard_map/ppermute | solution.py:18
  193.4 1.8 copy-start.2
  193.4 1.8 copy-start.8
  193.4 1.8 copy-start.9
Sparse Core Ops, SparseCore 0:
  57.9 50.5 all-gather.2
  110.4 50.1 all-gather.4
where the time goes:
time: 225 us; the launch traced here: 223 us
  blocking collectives  132 us (59%)
  local copies, waits for them, and re-layouts  50.2 us (22%)
  between operations  13.8 us (6%)
  starting transfers between devices  13.3 us (6%)
  matrix products  10 us (4%)
    all_gather x2, blocking collectives, conv_backward(): gathered = lax.all_gather(weights, 'dp', axis=1, tiled=True)  92.9 us
    another operation x20, local copies, waits for them, and re-layouts, conv_backward(): stacked = jnp.stack(shifted, axis=1)  36.9 us
    psum x2, blocking collectives, norm_backward(): lax.psum((group_sums(scaled), group_sums(scaled * normed)), 'rows')  26.5 us
    psum x1, blocking collectives, reduced_stats(): lax.psum((group_sums(values), group_sums(values * values)), 'rows')  12.3 us
    dot_general x2, matrix products, conv_backward(): result = jnp.dot(window, flat, preferred_element_type=jnp.float32)  10 us
    ppermute x2, starting transfers between devices, extended(): lax.ppermute(lax.slice_in_dim(block, 0, width, axis=dim), axis, backward)  9.26 us
    all_gather x2, local copies, waits for them, and re-layouts, conv_backward(): gathered = lax.all_gather(weights, 'dp', axis=1, tiled=True)  5.97 us
  transfers between devices with their start and end apart: 6, of which 2 were waited for; matrix products, arithmetic and copies ran while one was open for 23% of the time, Pallas kernels for 0%

commit v1 on v0

v1 whole, which is shorter than its diff:
```python
import functools

import jax
import jax.numpy as jnp
from jax import lax
from jax.experimental import pallas as pl
from jax.experimental.pallas import tpu as pltpu
from jax.sharding import PartitionSpec as P


GROUPS = 16
GSIZE = 40
LANES = 128


CHUNKS_TWO = ((0,), (1,), (2, 3))
CHUNKS_ONE = ((0, 1), (2, 3))

F32 = jnp.float32
BF16 = jnp.bfloat16


def up(number, unit):
    return -(-number // unit) * unit


def one_hot(source, target):
    return jnp.where(source == target, 1.0, 0.0).astype(BF16)


def dot(left, right):
    return jnp.dot(left, right, preferred_element_type=F32)


def iota(shape, axis):
    return lax.broadcasted_iota(jnp.int32, shape, axis)


class Plan:
    def __init__(self, images, width, channels):
        self.images, self.width, self.channels = images, width, channels
        self.height, self.planes = lax.axis_size("rows"), lax.axis_size("dp")
        self.rows = self.height * width
        self.blocks = self.height // images
        self.per_block = GROUPS // self.blocks
        self.number = float(self.rows * GSIZE)
        self.fast = (
            self.planes == 4 and images == 2 and self.blocks == 4 and self.per_block == self.planes
        )
        self.lanes = self.per_block * LANES
        self.field_lanes = up(2 * self.per_block * GSIZE, LANES)
        three = LANES // GSIZE
        self.mains = [
            list(range(start, min(start + three, self.per_block)))
            for start in range(0, self.per_block, three)
        ]
        self.spare = self.mains.pop()[0] if len(self.mains[-1]) == 1 else None

    def packed_rows(self, rows):
        return len(self.mains) * rows + (rows // 2 if self.spare is not None else 0)

    def place(self):
        here = lax.axis_index("rows")
        return lax.axis_index("dp"), here // self.images, here % self.images

    def channel(self, plane, block, order):
        if self.fast:
            return (order ^ plane) * (self.channels // self.planes) + block * GSIZE
        return (block * self.per_block + order) * GSIZE

    def targets(self, index, spans):
        target = jnp.full(index.shape, -1, jnp.int32)
        for start, channel in spans:
            inside = (index >= start) & (index < start + GSIZE)
            target = jnp.where(inside, channel + index - start, target)
        return target


def call(body, out, inputs, held=(), scratch=(), space=pltpu.VMEM):
    kinds = {pltpu.VMEM: pltpu.VMEM, pl.ANY: jax.ShapeDtypeStruct}
    outs = [kinds[space](shape, dtype) for shape, dtype in out]
    inputs = [
        pltpu.with_memory_space_constraint(value, pltpu.VMEM) if at in held else value
        for at, value in enumerate(inputs)
    ]
    vmem = pl.BlockSpec(memory_space=pltpu.VMEM)
    return pl.pallas_call(
        body,
        out_shape=outs,
        in_specs=[vmem] * len(inputs),
        out_specs=[vmem] * len(outs),
        scratch_shapes=list(scratch),
        compiler_params=pltpu.CompilerParams(vmem_limit_bytes=24 * 1024 * 1024),
    )(*inputs)


def pack_filters_kernel(first, second, *outs, plan):
    chunk = first.shape[2]
    position = plan.place()[1]
    for at, taps in enumerate((first, second)):
        parts = []
        for block in range(plan.blocks):
            rows = []
            for down in range(3):
                pieces = [
                    taps[3 * down + side, block * GSIZE : (block + 1) * GSIZE, :].astype(F32)
                    for side in range(3)
                ]
                pieces.append(jnp.zeros((LANES - 3 * GSIZE, chunk), F32))
                rows.append(jnp.concatenate(pieces, axis=0).T.astype(BF16))
            parts.append(rows)
        for step, out in enumerate(outs):
            wanted = position ^ step
            for down in range(3):
                value = parts[0][down]
                for block in range(1, plan.blocks):
                    value = jnp.where(wanted == block, parts[block][down], value)
                out[at, down] = value


def pack_fields_kernel(cotangent, hidden, latent, out, *, plan):
    plane = plan.place()[0]
    images, width, channels = cotangent.shape
    rows = iota((channels, 1), 0)
    lane = iota((1, plan.field_lanes), 1)
    own = plan.per_block * GSIZE
    for block in range(plan.blocks):
        mixed = jnp.zeros((images * width, plan.field_lanes), F32)
        for at, field in enumerate((hidden, latent)):
            spans = [
                (at * own + order * GSIZE, plan.channel(plane, block, order))
                for order in range(plan.per_block)
            ]
            select = one_hot(rows, plan.targets(lane, spans))
            mixed = mixed + dot(field[...].reshape(images * width, channels), select)
        mixed = mixed.astype(BF16).reshape(images, width, plan.field_lanes)
        for image in range(images):
            out[block * images + image, :, :channels] = cotangent[image]
            out[block * images + image, :, channels:] = mixed[image]


def group_total(values):
    return jnp.sum(jnp.sum(values, axis=0, keepdims=True), axis=1, keepdims=True)


def prepare_kernel(received, vectors, *outs, plan):
    padded, straight, main_table, spare_table = outs[:4]
    sides = (outs[4:7], outs[7:10])
    plane, position, _ = plan.place()
    width, channels, rows, lanes = plan.width, plan.channels, plan.rows, plan.lanes
    padded[:width, :] = jnp.zeros((width, channels), BF16)
    padded[width + rows :, :] = jnp.zeros((width, channels), BF16)
    field = received[:, :, :channels].reshape(rows, channels)
    padded[width : width + rows, :] = field
    lane = iota((1, lanes), 1)
    spans = [
        (order * LANES, plan.channel(plane, position, order)) for order in range(plan.per_block)
    ]
    straight[...] = dot(field, one_hot(iota((channels, 1), 0), plan.targets(lane, spans))).astype(BF16)
    own = plan.per_block * GSIZE
    fields = received[:, :, channels:].reshape(rows, plan.field_lanes)
    for at, (normed_out, factor_out, inverse_out) in enumerate(sides):
        spans = [(order * LANES, at * own + order * GSIZE) for order in range(plan.per_block)]
        select = one_hot(iota((plan.field_lanes, 1), 0), plan.targets(lane, spans))
        values = dot(fields, select)
        for order in range(plan.per_block):
            part = slice(order * LANES, (order + 1) * LANES)
            first = plan.channel(plane, position, order)
            gain = jnp.zeros((1, GSIZE), F32)
            shift = jnp.zeros((1, GSIZE), F32)
            for group in range(GROUPS):
                span = slice(group * GSIZE, (group + 1) * GSIZE)
                found = first == group * GSIZE
                gain = jnp.where(found, vectors[2 * at : 2 * at + 1, span], gain)
                shift = jnp.where(found, vectors[2 * at + 1 : 2 * at + 2, span], shift)
            rest = jnp.zeros((1, LANES - GSIZE), F32)
            gain = jnp.concatenate([gain, rest], axis=1)
            shift = jnp.concatenate([shift, rest], axis=1)
            block = values[:, part]
            average = group_total(block) / plan.number
            meansq = group_total(block * block) / plan.number
            inverse = lax.rsqrt(meansq - average * average + 1e-05)
            normed = (block - average) * inverse
            linear = normed * gain + shift
            logistic = 1.0 / (1.0 + jnp.exp(-linear))
            normed_out[:, part] = normed
            factor_out[:, part] = logistic * (1.0 + linear * (1.0 - logistic)) * gain
            inverse_out[:, part] = jnp.broadcast_to(inverse, (1, LANES))
    column = iota((1, channels), 1)
    row = iota((LANES, 1), 0)
    for step in range(plan.blocks):
        block = position ^ step
        for at, orders in enumerate(plan.mains):
            spans = [
                (local * GSIZE, plan.channel(plane, block, order))
                for local, order in enumerate(orders)
            ]
            main_table[at, step * LANES : (step + 1) * LANES, :] = one_hot(
                plan.targets(row, spans), column
            )
        if plan.spare is not None:
            for half in range(2):
                spans = [(half * GSIZE, plan.channel(plane, block, plan.spare))]
                spare_table[half, step * LANES : (step + 1) * LANES, :] = one_hot(
                    plan.targets(row, spans), column
                )


def load_weights(pieces, weights, plan):
    _, position, core = plan.place()
    for swap, by_order in enumerate(pieces):
        for order, arrays in enumerate(by_order):
            step = 0
            for array in arrays:
                for inner in range(array.shape[0]):
                    chunk = array.shape[2]
                    source = (position ^ step) * plan.images + (core ^ swap)
                    start = pl.multiple_of(source * chunk, 16)
                    weights[:, pl.ds(start, chunk), order * LANES : (order + 1) * LANES] = array[
                        inner
                    ]
                    step += 1


def convolve(padded, weights, width, part):
    rows = padded.shape[0] - 2 * width
    total = None
    for down in range(3):
        window = padded[(2 - down) * width : (2 - down) * width + rows, :]
        term = dot(window, weights[down, :, part])
        total = term if total is None else total + term
    return total


def fold_sides(total, width):
    rows = total.shape[0]
    column = lax.rem(iota((rows, 1), 0), width)
    first = jnp.where(column == width - 1, 0.0, pltpu.roll(total, rows - 1, 0))
    last = pltpu.roll(pltpu.roll(total, LANES - 2 * GSIZE, 1), 1, 0)
    last = jnp.where(column == 0, 0.0, last)
    return first + pltpu.roll(total, LANES - GSIZE, 1) + last


def norm_backward(incoming, normed, factor, inverse, number):
    scaled = incoming * factor
    first = group_total(scaled) / number
    second = group_total(scaled * normed) / number
    grad = inverse * (scaled - first - normed * second)
    return jnp.where(iota((1, LANES), 1) < GSIZE, grad, 0.0)


def side_by_side(parts):
    total = parts[0]
    for at, part in enumerate(parts[1:]):
        total = total + pltpu.roll(part, (at + 1) * GSIZE, 1)
    return total.astype(BF16)


def block_backward(padded, weights, normed, factor, inverse, plan):
    grads = []
    pair = 2 if plan.per_block % 2 == 0 else 1
    for start in range(0, plan.per_block, pair):
        total = convolve(padded, weights, plan.width, slice(start * LANES, (start + pair) * LANES))
        for at in range(pair):
            part = slice((start + at) * LANES, (start + at + 1) * LANES)
            incoming = fold_sides(total[:, at * LANES : (at + 1) * LANES], plan.width)
            grads.append(
                norm_backward(incoming, normed[:, part], factor[:, part], inverse[:, part], plan.number)
            )
    return grads


def hidden_kernel(padded, normed, factor, inverse, *rest, layout, plan):
    out, weights = rest[layout.total :]
    layout.fill(rest[: layout.total], weights, plan)
    grads = block_backward(padded, weights, normed, factor, inverse, plan)
    rows, half = plan.rows, plan.rows // 2
    for at, orders in enumerate(plan.mains):
        out[at * rows : (at + 1) * rows, :] = side_by_side([grads[order] for order in orders])
    if plan.spare is not None:
        grad = grads[plan.spare]
        out[len(plan.mains) * rows :, :] = side_by_side([grad[:half], grad[half:]])


def unpack(pieces, main_table, spare_table, rows, plan):
    total = None
    for at in range(len(plan.mains)):
        wide = jnp.concatenate([piece[at * rows : (at + 1) * rows, :] for piece in pieces], axis=1)
        term = dot(wide, main_table[at])
        total = term if total is None else total + term
    halves = [None, None] if total is None else [total[: rows // 2], total[rows // 2 :]]
    if plan.spare is not None:
        base = len(plan.mains) * rows
        wide = jnp.concatenate([piece[base : base + rows // 2, :] for piece in pieces], axis=1)
        for half in range(2):
            term = dot(wide, spare_table[half])
            halves[half] = term if halves[half] is None else halves[half] + term
    return [half.astype(BF16) for half in halves]


def latent_kernel(straight, main_table, spare_table, normed, factor, inverse, *rest, layout, plan):
    blocks = plan.blocks
    pieces = rest[:blocks]
    out, weights, padded = rest[blocks + layout.total :]
    layout.fill(rest[blocks : blocks + layout.total], weights, plan)
    width, rows, half = plan.width, plan.rows, plan.rows // 2
    padded[:width, :] = jnp.zeros((width, plan.channels), BF16)
    padded[width + rows :, :] = jnp.zeros((width, plan.channels), BF16)
    low, high = unpack(pieces, main_table, spare_table, rows, plan)
    padded[width : width + half, :] = low
    padded[width + half : width + rows, :] = high
    grads = block_backward(padded, weights, normed, factor, inverse, plan)
    for order in range(plan.per_block):
        grads[order] = straight[:, order * LANES : (order + 1) * LANES].astype(F32) + grads[order]
    for at, orders in enumerate(plan.mains):
        value = side_by_side([grads[order] for order in orders])
        out[:, at * width : (at + 1) * width, :] = value.reshape(plan.height, width, LANES)
    if plan.spare is not None:
        grad = grads[plan.spare].reshape(plan.height, width, LANES)
        parts = [
            grad[:, at * width // 2 : (at + 1) * width // 2, :].reshape(half, LANES) for at in range(2)
        ]
        value = side_by_side(parts).reshape(plan.height, width // 2, LANES)
        out[:, len(plan.mains) * width :, :] = value


def spread_kernel(received, main_table, spare_table, out, *, plan):
    position = plan.place()[1]
    for image in range(plan.images):
        pieces = [
            received[(position ^ step) * plan.images + image] for step in range(plan.blocks)
        ]
        low, high = unpack(pieces, main_table, spare_table, plan.width, plan)
        out[image, : plan.width // 2, :] = low
        out[image, plan.width // 2 :, :] = high


class Layout:
    def __init__(self, pieces):
        self.dynamic = isinstance(pieces, list)
        if self.dynamic:
            self.counts = [[len(arrays) for arrays in by_order] for by_order in pieces]
            self.flat = [array for by_order in pieces for arrays in by_order for array in arrays]
        else:
            self.flat = [pieces]
        self.total = len(self.flat)

    def fill(self, flat, weights, plan):
        if not self.dynamic:
            weights[...] = flat[0][...]
            return
        flat, nested = list(flat), []
        for counts in self.counts:
            nested.append([[flat.pop(0) for _ in range(count)] for count in counts])
        load_weights(nested, weights, plan)


def flip(array, axis, mask):
    return lax.ppermute(array, axis, [(i, i ^ mask) for i in range(lax.axis_size(axis))])


def plane_pieces(filter_two, filter_one, plan):
    out = [((2, 3, filter_two.shape[2], LANES), BF16)] * plan.blocks
    mine = call(functools.partial(pack_filters_kernel, plan=plan), out, [filter_two, filter_one])
    return [mine[0]] + [
        flip(mine[turn], "rows", turn * plan.images) for turn in range(1, plan.blocks)
    ]


def gathered_filter(mine, chunks):
    own = [jnp.stack([mine[turn] for turn in chunk]) for chunk in chunks]
    far = [flip(piece, "dp", 2) for piece in own]
    near = [flip(piece, "dp", 1) for piece in own]
    last = [flip(piece, "dp", 1) for piece in far]
    orders = [own, near, far, last]
    swapped = [[flip(piece, "rows", 1) for piece in order] for order in orders]
    return [orders, swapped]


def assembled_filter(taps, plan):
    count, _, chunk = taps.shape
    blocks, per_block, sources = plan.blocks, plan.per_block, plan.height
    whole = lax.all_gather(taps, "dp", axis=1, tiled=True)
    whole = whole.reshape(count, blocks, per_block * GSIZE, chunk)
    whole = jnp.repeat(jnp.moveaxis(whole, 1, 0), plan.images, axis=0)
    whole = lax.all_to_all(whole, "rows", 0, 0, tiled=True)
    whole = whole.reshape(sources, 3, 3, per_block, GSIZE, chunk)
    whole = jnp.transpose(whole, (1, 0, 5, 3, 2, 4)).reshape(3, sources * chunk, per_block, 3 * GSIZE)
    whole = jnp.pad(whole, ((0, 0), (0, 0), (0, 0), (0, LANES - 3 * GSIZE)))
    return whole.reshape(3, sources * chunk, per_block * LANES)


def step(
    latent, hidden, cotangent, filter_one, filter_two, gain_one, shift_one, gain_two, shift_two
):
    images, _, width, channels = latent.shape
    plan = Plan(images, width, channels)
    rows, lanes = plan.rows, plan.lanes

    if plan.fast:
        mine = plane_pieces(filter_two, filter_one, plan)
        two = Layout(gathered_filter([piece[0] for piece in mine], CHUNKS_TWO))
        one = Layout(gathered_filter([piece[1] for piece in mine], CHUNKS_ONE))
    else:
        two = Layout(assembled_filter(filter_two, plan))
        one = Layout(assembled_filter(filter_one, plan))
    (sent,) = call(
        functools.partial(pack_fields_kernel, plan=plan),
        [((plan.height, width, channels + plan.field_lanes), BF16)],
        [cotangent[:, 0], hidden[:, 0], latent[:, 0]],
    )
    received = lax.all_to_all(sent, "rows", 0, 0, tiled=True)
    vectors = jnp.stack([gain_two, shift_two, gain_one, shift_one])
    table = plan.blocks * LANES
    side = [((rows, lanes), F32), ((rows, lanes), F32), ((1, lanes), F32)]
    prepared = call(
        functools.partial(prepare_kernel, plan=plan),
        [
            ((rows + 2 * width, channels), BF16),
            ((rows, lanes), BF16),
            ((max(len(plan.mains), 1), table, channels), BF16),
            ((2, table, channels), BF16),
        ]
        + side
        + side,
        [received, vectors],
    )
    padded, straight, main_table, spare_table = prepared[:4]
    weights = pltpu.VMEM((3, channels, lanes), BF16)
    inputs = [padded, *prepared[4:7], *two.flat]
    (grad,) = call(
        functools.partial(hidden_kernel, layout=two, plan=plan),
        [((plan.packed_rows(rows), LANES), BF16)],
        inputs,
        held=range(len(inputs)),
        scratch=[weights],
    )
    grads = [grad] + [flip(grad, "rows", turn * images) for turn in range(1, plan.blocks)]
    inputs = [straight, main_table, spare_table, *prepared[7:10], *grads, *one.flat]
    (result,) = call(
        functools.partial(latent_kernel, layout=one, plan=plan),
        [((plan.height, plan.packed_rows(width), LANES), BF16)],
        inputs,
        held=range(len(inputs)),
        scratch=[weights, pltpu.VMEM((rows + 2 * width, channels), BF16)],
    )
    result = lax.all_to_all(result, "rows", 0, 0, tiled=True)
    (out,) = call(
        functools.partial(spread_kernel, plan=plan),
        [((images, width, channels), BF16)],
        [result, main_table, spare_table],
        held=(1, 2),
        space=pl.ANY,
    )
    return out[:, None]


def solution(mesh):
    in_specs = (
        P("dp", "rows", None, None),
        P("dp", "rows", None, None),
        P("dp", "rows", None, None),
        P(None, "dp", "rows"),
        P(None, "dp", "rows"),
        P(),
        P(),
        P(),
        P(),
    )
    out_specs = P("dp", "rows", None, None)
    return jax.shard_map(step, mesh=mesh, in_specs=in_specs, out_specs=out_specs, check_vma=False)
```

time: 225 us -> 119 us (0.53)
  the two profiles are of different devices: /device:TPU:28 before, /device:TPU:0 now
where the time goes in v1:
time: 119 us; the launch traced here: 118 us
  waiting for transfers between devices  41.9 us (35%)
  starting transfers between devices  34.1 us (29%)
  local copies, waits for them, and re-layouts  18.9 us (16%)
  Pallas kernels  14.1 us (12%)
  blocking collectives  8.6 us (7%)
    ppermute x41, waiting for transfers between devices, flip(): lax.ppermute(array, axis, [(i, i ^ mask) for i in range(lax.axis_size(axi...  41.9 us
    ppermute x41, starting transfers between devices, flip(): lax.ppermute(array, axis, [(i, i ^ mask) for i in range(lax.axis_size(axi...  30.4 us
    unnamed x74, local copies, waits for them, and re-layouts  18.8 us
    pallas_call x6, Pallas kernels, call(): pl.pallas_call(body, out_shape=outs, in_specs=[vmem] * len(inputs), out_s...  14.1 us
    all_to_all x1, blocking collectives, step(): result = lax.all_to_all(result, 'rows', 0, 0, tiled=True)  8.6 us
    all_to_all x1, starting transfers between devices, step(): received = lax.all_to_all(sent, 'rows', 0, 0, tiled=True)  3.7 us
  transfers between devices with their start and end apart: 42, of which 14 were waited for; matrix products, arithmetic and copies ran while one was open for 0% of the time, Pallas kernels for 7%

profile of v1, /device:TPU:0, one launch (start us, length us, event | category | flops | bytes accessed | tf_op | source)
XLA Modules:
  0.0 117.9 jit_solution(15455122121440756459)
XLA Ops:
  0.0 1.0 copy-done
  1.0 1.0 copy-done.1
  2.3 3.0 %collective-permute-start = (bf16[2,3,80,128]{3,2,1,0:T(8,128)(2,1)S(1)}, bf16[2,3,80,128]{3,2,1,0:T(8,128)(2,1)S(1)}, u32[]{:S(2)}, u32[]{:S(2)}) collective-permute-start(bf16[2,3,80,128]{3,2,1,0:T(8,128)(2,1)S(1)} %get-tuple-element.30), channel_id=1, source_target_pairs={{0,2},{1,3},{2,0},{3,1},{4,6},{5,7},{6,4},{7,5},{8,10},{9,11},{10,... | collective-permute-start | bytes 368648 | tf_op jit(solution)/shard_map/ppermute | solution.py:359
  5.3 2.7 %collective-permute-start.6 = (bf16[1,3,80,128]{3,2,1,0:T(8,128)(2,1)S(1)}, bf16[1,3,80,128]{3,2,1,0:T(8,128)(2,1)S(1)}, u32[]{:S(2)}, u32[]{:S(2)}) collective-permute-start(bf16[1,3,80,128]{3,2,1,0:T(8,128)(2,1)S(1)} %get-tuple-element.38.rest_0_), channel_id=1, source_target_pairs={{0,16},{8,24},{16,0},{24,8},{1,17},{9,25},{17,1},{25,9},{2,18},{10... | collective-permute-start | bytes 184328 | tf_op jit(solution)/shard_map/ppermute | solution.py:359
  8.0 1.6 %collective-permute-start.3 = (bf16[1,3,80,128]{3,2,1,0:T(8,128)(2,1)S(1)}, bf16[1,3,80,128]{3,2,1,0:T(8,128)(2,1)S(1)}, u32[]{:S(2)}, u32[]{:S(2)}) collective-permute-start(bf16[1,3,80,128]{3,2,1,0:T(8,128)(2,1)S(1)} %get-tuple-element.38.rest_0_), channel_id=1, source_target_pairs={{0,8},{8,0},{16,24},{24,16},{1,9},{9,1},{17,25},{25,17},{2,10},{10... | collective-permute-start | bytes 184328 | tf_op jit(solution)/shard_map/ppermute | solution.py:359
  9.5 0.9 copy-done.2
  12.3 1.9 %shard_map.91 = bf16[8,64,1024]{2,1,0:T(8,128)(2,1)} custom-call(bf16[2,64,640]{2,1,0:T(8,128)(2,1)S(1)} %bitcast.6, bf16[2,64,640]{2,1,0:T(8,128)(2,1)S(1)} %bitcast.7, bf16[2,64,640]{2,1,0:T(8,128)(2,1)S(1)} %bitcast.8), custom_call_target="tpu_custom_call" | custom-call | tf_op jit(solution)/shard_map/pallas_call | solution.py:87
  14.2 3.7 %all-to-all-start = ((bf16[8,64,1024]{2,1,0:T(8,128)(2,1)}), bf16[8,64,1024]{2,1,0:T(8,128)(2,1)S(1)}, u32[]{:S(2)}, u32[]{:S(2)}) async-start(bf16[8,64,1024]{2,1,0:T(8,128)(2,1)} %shard_map.91), calls=%async_computation | async-start | bytes 2097152 | tf_op jit(solution)/shard_map/all_to_all | solution.py:412
  17.9 2.9 %collective-permute-start.2 = (bf16[2,3,80,128]{3,2,1,0:T(8,128)(2,1)S(1)}, bf16[2,3,80,128]{3,2,1,0:T(8,128)(2,1)S(1)}, u32[]{:S(2)}, u32[]{:S(2)}) collective-permute-start(bf16[2,3,80,128]{3,2,1,0:T(8,128)(2,1)S(1)} %get-tuple-element.32), channel_id=1, source_target_pairs={{0,6},{1,7},{2,4},{3,5},{4,2},{5,3},{6,0},{7,1},{8,14},{9,15},{10,... | collective-permute-start | bytes 368648 | tf_op jit(solution)/shard_map/ppermute | solution.py:359
  21.9 14.1 %collective-permute-done.2 = bf16[2,3,80,128]{3,2,1,0:T(8,128)(2,1)S(1)} collective-permute-done((bf16[2,3,80,128]{3,2,1,0:T(8,128)(2,1)S(1)}, bf16[2,3,80,128]{3,2,1,0:T(8,128)(2,1)S(1)}, u32[]{:S(2)}, u32[]{:S(2)}) %collective-permute-start.2) | collective-permute-done | bytes 122912 | tf_op jit(solution)/shard_map/ppermute | solution.py:359
  36.0 1.6 %collective-permute-done.1 = bf16[2,3,80,128]{3,2,1,0:T(8,128)(2,1)S(1)} collective-permute-done((bf16[2,3,80,128]{3,2,1,0:T(8,128)(2,1)S(1)}, bf16[2,3,80,128]{3,2,1,0:T(8,128)(2,1)S(1)}, u32[]{:S(2)}, u32[]{:S(2)}) %collective-permute-start.1) | collective-permute-done | bytes 122912 | tf_op jit(solution)/shard_map/ppermute | solution.py:359
  38.5 1.6 %collective-permute-start.5 = (bf16[2,3,80,128]{3,2,1,0:T(8,128)(2,1)S(1)}, bf16[2,3,80,128]{3,2,1,0:T(8,128)(2,1)S(1)}, u32[]{:S(2)}, u32[]{:S(2)}) collective-permute-start(bf16[2,3,80,128]{3,2,1,0:T(8,128)(2,1)S(1)} %pad_maximum_fusion.rest_2_), channel_id=1, source_target_pairs={{0,8},{8,0},{16,24},{24,16},{1,9},{9,1},{17,25},{25,17},{2,10},{10... | collective-permute-start | bytes 368648 | tf_op jit(solution)/shard_map/ppermute | solution.py:359
  40.0 2.6 %collective-permute-start.8 = (bf16[2,3,80,128]{3,2,1,0:T(8,128)(2,1)S(1)}, bf16[2,3,80,128]{3,2,1,0:T(8,128)(2,1)S(1)}, u32[]{:S(2)}, u32[]{:S(2)}) collective-permute-start(bf16[2,3,80,128]{3,2,1,0:T(8,128)(2,1)S(1)} %pad_maximum_fusion.rest_2_), channel_id=1, source_target_pairs={{0,16},{8,24},{16,0},{24,8},{1,17},{9,25},{17,1},{25,9},{2,18},{10... | collective-permute-start | bytes 368648 | tf_op jit(solution)/shard_map/ppermute | solution.py:359
  42.6 1.7 %collective-permute-done.4.rest_4_ = bf16[1,3,80,128]{3,2,1,0:T(8,128)(2,1)S(1)} collective-permute-done((bf16[1,3,80,128]{3,2,1,0:T(8,128)(2,1)S(1)}, bf16[1,3,80,128]{3,2,1,0:T(8,128)(2,1)S(1)}, u32[]{:S(2)}, u32[]{:S(2)}) %collective-permute-start.4) | collective-permute-done | bytes 61472 | tf_op jit(solution)/shard_map/ppermute | solution.py:359
  45.7 1.3 %collective-permute-start.10 = (bf16[1,3,80,128]{3,2,1,0:T(8,128)(2,1)S(1)}, bf16[1,3,80,128]{3,2,1,0:T(8,128)(2,1)S(1)}, u32[]{:S(2)}, u32[]{:S(2)}) collective-permute-start(bf16[1,3,80,128]{3,2,1,0:T(8,128)(2,1)S(1)} %collective-permute-done.7.rest_7_), channel_id=1, source_target_pairs={{0,8},{8,0},{16,24},{24,16},{1,9},{9,1},{17,25},{25,17},{2,10},{10... | collective-permute-start | bytes 184328 | tf_op jit(solution)/shard_map/ppermute | solution.py:359
  47.8 1.2 collective-permute-done.8.rest_8_
  49.0 3.7 %collective-permute-done.10.rest_10_ = bf16[1,3,80,128]{3,2,1,0:T(8,128)(2,1)S(1)} collective-permute-done((bf16[1,3,80,128]{3,2,1,0:T(8,128)(2,1)S(1)}, bf16[1,3,80,128]{3,2,1,0:T(8,128)(2,1)S(1)}, u32[]{:S(2)}, u32[]{:S(2)}) %collective-permute-start.10) | collective-permute-done | bytes 61472 | tf_op jit(solution)/shard_map/ppermute | solution.py:359
  52.7 1.2 %collective-permute-start.29 = (bf16[2,3,80,128]{3,2,1,0:T(8,128)(2,1)S(1)}, bf16[2,3,80,128]{3,2,1,0:T(8,128)(2,1)S(1)}, u32[]{:S(2)}, u32[]{:S(2)}) collective-permute-start(bf16[2,3,80,128]{3,2,1,0:T(8,128)(2,1)S(1)} %pad_maximum_fusion.1.rest_4_), channel_id=1, source_target_pairs={{0,16},{8,24},{16,0},{24,8},{1,17},{9,25},{17,1},{25,9},{2,18},{10... | collective-permute-start | bytes 368648 | tf_op jit(solution)/shard_map/ppermute | solution.py:359
  54.5 1.7 %collective-permute-start.30 = (bf16[2,3,80,128]{3,2,1,0:T(8,128)(2,1)S(1)}, bf16[2,3,80,128]{3,2,1,0:T(8,128)(2,1)S(1)}, u32[]{:S(2)}, u32[]{:S(2)}) collective-permute-start(bf16[2,3,80,128]{3,2,1,0:T(8,128)(2,1)S(1)} %pad_maximum_fusion.2.rest_5_), channel_id=1, source_target_pairs={{0,16},{8,24},{16,0},{24,8},{1,17},{9,25},{17,1},{25,9},{2,18},{10... | collective-permute-start | bytes 368648 | tf_op jit(solution)/shard_map/ppermute | solution.py:359
  57.7 7.0 %collective-permute-done.29.rest_8_ = bf16[2,3,80,128]{3,2,1,0:T(8,128)(2,1)S(1)} collective-permute-done((bf16[2,3,80,128]{3,2,1,0:T(8,128)(2,1)S(1)}, bf16[2,3,80,128]{3,2,1,0:T(8,128)(2,1)S(1)}, u32[]{:S(2)}, u32[]{:S(2)}) %collective-permute-start.29) | collective-permute-done | bytes 122912 | tf_op jit(solution)/shard_map/ppermute | solution.py:359
  64.7 2.6 %collective-permute-done.30.rest_9_ = bf16[2,3,80,128]{3,2,1,0:T(8,128)(2,1)S(1)} collective-permute-done((bf16[2,3,80,128]{3,2,1,0:T(8,128)(2,1)S(1)}, bf16[2,3,80,128]{3,2,1,0:T(8,128)(2,1)S(1)}, u32[]{:S(2)}, u32[]{:S(2)}) %collective-permute-start.30) | collective-permute-done | bytes 122912 | tf_op jit(solution)/shard_map/ppermute | solution.py:359
  69.9 1.5 %collective-permute-start.32 = (bf16[2,3,80,128]{3,2,1,0:T(8,128)(2,1)S(1)}, bf16[2,3,80,128]{3,2,1,0:T(8,128)(2,1)S(1)}, u32[]{:S(2)}, u32[]{:S(2)}) collective-permute-start(bf16[2,3,80,128]{3,2,1,0:T(8,128)(2,1)S(1)} %collective-permute-done.30.rest_9_), channel_id=1, source_target_pairs={{0,8},{8,0},{16,24},{24,16},{1,9},{9,1},{17,25},{25,17},{2,10},{10... | collective-permute-start | bytes 368648 | tf_op jit(solution)/shard_map/ppermute | solution.py:359
  72.0 1.2 %collective-permute-done.31.rest_10_ = bf16[2,3,80,128]{3,2,1,0:T(8,128)(2,1)S(1)} collective-permute-done((bf16[2,3,80,128]{3,2,1,0:T(8,128)(2,1)S(1)}, bf16[2,3,80,128]{3,2,1,0:T(8,128)(2,1)S(1)}, u32[]{:S(2)}, u32[]{:S(2)}) %collective-permute-start.31) | collective-permute-done | bytes 122912 | tf_op jit(solution)/shard_map/ppermute | solution.py:359
  73.7 3.1 %shard_map.92 = (bf16[640,640]{1,0:T(8,128)(2,1)S(1)}, bf16[512,512]{1,0:T(8,128)(2,1)S(1)}, bf16[1,512,640]{2,1,0:T(8,128)(2,1)S(1)}, bf16[2,512,640]{2,1,0:T(8...) custom-call(bf16[8,64,1024]{2,1,0:T(8,128)(2,1)S(1)} %all-to-all-don, ...), custom_call_target="tpu_custom_call" | custom-call | tf_op jit(solution)/shard_map/pallas_call | solution.py:87
  88.4 2.7 %shard_map.94.rest_0_ = bf16[768,128]{1,0:T(8,128)(2,1)S(1)} custom-call(bf16[640,640]{1,0:T(8,128)(2,1)S(1)} %get-tuple-element.25.padded, f32[512,512]{1,0:T(8,128)S(1)} %get-tuple-element.26.normed, f32[512,512]{1,0:T(8,128)S(1)} %get-tuple-element.27.factor, f32[1,512]{1,0:T(1,128)S(1)} %get-tuple-element.28.inverse, ...), custom_call_target="tpu_custom_call" | custom-call | tf_op jit(solution)/shard_map/pallas_call | solution.py:87
  91.1 1.3 %collective-permute-start.24 = (bf16[768,128]{1,0:T(8,128)(2,1)S(1)}, bf16[768,128]{1,0:T(8,128)(2,1)S(1)}, u32[]{:S(2)}, u32[]{:S(2)}) collective-permute-start(bf16[768,128]{1,0:T(8,128)(2,1)S(1)} %shard_map.94.rest_0_), channel_id=1, source_target_pairs={{0,2},{1,3},{2,0},{3,1},{4,6},{5,7},{6,4},{7,5},{8,10},{9,11},{10,... | collective-permute-start | bytes 589832 | tf_op jit(solution)/shard_map/ppermute | solution.py:359
  92.8 1.9 %collective-permute-start.26 = (bf16[768,128]{1,0:T(8,128)(2,1)S(1)}, bf16[768,128]{1,0:T(8,128)(2,1)S(1)}, u32[]{:S(2)}, u32[]{:S(2)}) collective-permute-start(bf16[768,128]{1,0:T(8,128)(2,1)S(1)} %shard_map.94.rest_0_), channel_id=1, source_target_pairs={{0,6},{1,7},{2,4},{3,5},{4,2},{5,3},{6,0},{7,1},{8,14},{9,15},{10,... | collective-permute-start | bytes 589832 | tf_op jit(solution)/shard_map/ppermute | solution.py:359
  96.2 2.8 %collective-permute-done.24.rest_1_ = bf16[768,128]{1,0:T(8,128)(2,1)S(1)} collective-permute-done((bf16[768,128]{1,0:T(8,128)(2,1)S(1)}, bf16[768,128]{1,0:T(8,128)(2,1)S(1)}, u32[]{:S(2)}, u32[]{:S(2)}) %collective-permute-start.24) | collective-permute-done | bytes 196640 | tf_op jit(solution)/shard_map/ppermute | solution.py:359
  98.9 4.2 %collective-permute-done.25.rest_2_ = bf16[768,128]{1,0:T(8,128)(2,1)S(1)} collective-permute-done((bf16[768,128]{1,0:T(8,128)(2,1)S(1)}, bf16[768,128]{1,0:T(8,128)(2,1)S(1)}, u32[]{:S(2)}, u32[]{:S(2)}) %collective-permute-start.25) | collective-permute-done | bytes 196640 | tf_op jit(solution)/shard_map/ppermute | solution.py:359
  103.1 4.7 %shard_map.95 = bf16[8,96,128]{2,1,0:T(8,128)(2,1)S(1)} custom-call(bf16[512,512]{1,0:T(8,128)(2,1)S(1)} %get-tuple-element.19.straight, bf16[1,512,640]{2,1,0:T(8,128)(2,1)S(1)} %get-tuple-element.20.main_table, bf16[2,512,640]{2,1,0:T(8,128)(2,1)S(1)} %get-tuple-element.21.spare_table, f32[512,512]{1,0:T(8,128)S(1)} %get-tuple-element.22.normed, ...), custom_call_target="tpu_custom_call" | custom-call | tf_op jit(solution)/shard_map/pallas_call | solution.py:87
  107.8 8.6 %all_to_all.10.received = bf16[8,96,128]{2,1,0:T(8,128)(2,1)S(1)} all-to-all(bf16[8,96,128]{2,1,0:T(8,128)(2,1)S(1)} %shard_map.95), channel_id=1, replica_groups=mesh['dp'=4,'rows'=8] {'rows'}, dimensions={0} | all-to-all | bytes 393216 | tf_op jit(solution)/shard_map/all_to_all | solution.py:447
  116.4 1.5 %shard_map.96 = bf16[2,64,640]{2,1,0:T(8,128)(2,1)} custom-call(bf16[8,96,128]{2,1,0:T(8,128)(2,1)S(1)} %all_to_all.10.received, bf16[1,512,640]{2,1,0:T(8,128)(2,1)S(1)} %get-tuple-element.20.main_table, bf16[2,512,640]{2,1,0:T(8,128)(2,1)S(1)} %get-tuple-element.21.spare_table), custom_call_target="tpu_custom_call" | custom-call | tf_op jit(solution)/shard_map/pallas_call | solution.py:87
  (145 shorter events, 25.5 us)
Async XLA Ops:
  2.3 19.1 %collective-permute-start = (bf16[2,3,80,128]{3,2,1,0:T(8,128)(2,1)S(1)}, bf16[2,3,80,128]{3,2,1,0:T(8,128)(2,1)S(1)}, u32[]{:S(2)}, u32[]{:S(2)}) collective-permute-start(bf16[2,3,80,128]{3,2,1,0:T(8,128)(2,1)S(1)} %get-tuple-element.30), channel_id=1, source_target_pairs={{0,2},{1,3},{2,0},{3,1},{4,6},{5,7},{6,4},{7,5},{8,10},{9,11},{10,... | collective-permute-start | bytes 368648 | tf_op jit(solution)/shard_map/ppermute | solution.py:359
  5.3 15.5 %collective-permute-start.6 = (bf16[1,3,80,128]{3,2,1,0:T(8,128)(2,1)S(1)}, bf16[1,3,80,128]{3,2,1,0:T(8,128)(2,1)S(1)}, u32[]{:S(2)}, u32[]{:S(2)}) collective-permute-start(bf16[1,3,80,128]{3,2,1,0:T(8,128)(2,1)S(1)} %get-tuple-element.38.rest_0_), channel_id=1, source_target_pairs={{0,16},{8,24},{16,0},{24,8},{1,17},{9,25},{17,1},{25,9},{2,18},{10... | collective-permute-start | bytes 184328 | tf_op jit(solution)/shard_map/ppermute | solution.py:359
  8.0 13.8 %collective-permute-start.3 = (bf16[1,3,80,128]{3,2,1,0:T(8,128)(2,1)S(1)}, bf16[1,3,80,128]{3,2,1,0:T(8,128)(2,1)S(1)}, u32[]{:S(2)}, u32[]{:S(2)}) collective-permute-start(bf16[1,3,80,128]{3,2,1,0:T(8,128)(2,1)S(1)} %get-tuple-element.38.rest_0_), channel_id=1, source_target_pairs={{0,8},{8,0},{16,24},{24,16},{1,9},{9,1},{17,25},{25,17},{2,10},{10... | collective-permute-start | bytes 184328 | tf_op jit(solution)/shard_map/ppermute | solution.py:359
  9.5 28.5 %collective-permute-start.12 = (bf16[1,3,80,128]{3,2,1,0:T(8,128)(2,1)S(1)}, bf16[1,3,80,128]{3,2,1,0:T(8,128)(2,1)S(1)}, u32[]{:S(2)}, u32[]{:S(2)}) collective-permute-start(bf16[1,3,80,128]{3,2,1,0:T(8,128)(2,1)S(1)} %get-tuple-element.38.rest_0_), channel_id=1, source_target_pairs={{0,1},{1,0},{2,3},{3,2},{4,5},{5,4},{6,7},{7,6},{8,9},{9,8},{10,11... | collective-permute-start | bytes 184328 | tf_op jit(solution)/shard_map/ppermute | solution.py:359
  14.2 59.5 %all-to-all-start = ((bf16[8,64,1024]{2,1,0:T(8,128)(2,1)}), bf16[8,64,1024]{2,1,0:T(8,128)(2,1)S(1)}, u32[]{:S(2)}, u32[]{:S(2)}) async-start(bf16[8,64,1024]{2,1,0:T(8,128)(2,1)} %shard_map.91), calls=%async_computation | async-start | bytes 2097152 | tf_op jit(solution)/shard_map/all_to_all | solution.py:412
  17.9 18.0 %collective-permute-start.2 = (bf16[2,3,80,128]{3,2,1,0:T(8,128)(2,1)S(1)}, bf16[2,3,80,128]{3,2,1,0:T(8,128)(2,1)S(1)}, u32[]{:S(2)}, u32[]{:S(2)}) collective-permute-start(bf16[2,3,80,128]{3,2,1,0:T(8,128)(2,1)S(1)} %get-tuple-element.32), channel_id=1, source_target_pairs={{0,6},{1,7},{2,4},{3,5},{4,2},{5,3},{6,0},{7,1},{8,14},{9,15},{10,... | collective-permute-start | bytes 368648 | tf_op jit(solution)/shard_map/ppermute | solution.py:359
  20.8 16.8 %collective-permute-start.1 = (bf16[2,3,80,128]{3,2,1,0:T(8,128)(2,1)S(1)}, bf16[2,3,80,128]{3,2,1,0:T(8,128)(2,1)S(1)}, u32[]{:S(2)}, u32[]{:S(2)}) collective-permute-start(bf16[2,3,80,128]{3,2,1,0:T(8,128)(2,1)S(1)} %get-tuple-element.31), channel_id=1, source_target_pairs={{0,4},{1,5},{2,6},{3,7},{4,0},{5,1},{6,2},{7,3},{8,12},{9,13},{10,... | collective-permute-start | bytes 368648 | tf_op jit(solution)/shard_map/ppermute | solution.py:359
  21.3 17.1 %collective-permute-start.9 = (bf16[1,3,80,128]{3,2,1,0:T(8,128)(2,1)S(1)}, bf16[1,3,80,128]{3,2,1,0:T(8,128)(2,1)S(1)}, u32[]{:S(2)}, u32[]{:S(2)}) collective-permute-start(bf16[1,3,80,128]{3,2,1,0:T(8,128)(2,1)S(1)} %collective-permute-done.6.rest_6_), channel_id=1, source_target_pairs={{0,8},{8,0},{16,24},{24,16},{1,9},{9,1},{17,25},{25,17},{2,10},{10... | collective-permute-start | bytes 184328 | tf_op jit(solution)/shard_map/ppermute | solution.py:359
  21.8 20.8 %collective-permute-start.18 = (bf16[1,3,80,128]{3,2,1,0:T(8,128)(2,1)S(1)}, bf16[1,3,80,128]{3,2,1,0:T(8,128)(2,1)S(1)}, u32[]{:S(2)}, u32[]{:S(2)}) collective-permute-start(bf16[1,3,80,128]{3,2,1,0:T(8,128)(2,1)S(1)} %collective-permute-done.6.rest_6_), channel_id=1, source_target_pairs={{0,1},{1,0},{2,3},{3,2},{4,5},{5,4},{6,7},{7,6},{8,9},{9,8},{10,11... | collective-permute-start | bytes 184328 | tf_op jit(solution)/shard_map/ppermute | solution.py:359
  37.5 6.8 %collective-permute-start.4 = (bf16[1,3,80,128]{3,2,1,0:T(8,128)(2,1)S(1)}, bf16[1,3,80,128]{3,2,1,0:T(8,128)(2,1)S(1)}, u32[]{:S(2)}, u32[]{:S(2)}) collective-permute-start(bf16[1,3,80,128]{3,2,1,0:T(8,128)(2,1)S(1)} %get-tuple-element.40.rest_1_), channel_id=1, source_target_pairs={{0,8},{8,0},{16,24},{24,16},{1,9},{9,1},{17,25},{25,17},{2,10},{10... | collective-permute-start | bytes 184328 | tf_op jit(solution)/shard_map/ppermute | solution.py:359
  38.1 6.3 %collective-permute-start.7 = (bf16[1,3,80,128]{3,2,1,0:T(8,128)(2,1)S(1)}, bf16[1,3,80,128]{3,2,1,0:T(8,128)(2,1)S(1)}, u32[]{:S(2)}, u32[]{:S(2)}) collective-permute-start(bf16[1,3,80,128]{3,2,1,0:T(8,128)(2,1)S(1)} %get-tuple-element.40.rest_1_), channel_id=1, source_target_pairs={{0,16},{8,24},{16,0},{24,8},{1,17},{9,25},{17,1},{25,9},{2,18},{10... | collective-permute-start | bytes 184328 | tf_op jit(solution)/shard_map/ppermute | solution.py:359
  38.5 8.5 %collective-permute-start.5 = (bf16[2,3,80,128]{3,2,1,0:T(8,128)(2,1)S(1)}, bf16[2,3,80,128]{3,2,1,0:T(8,128)(2,1)S(1)}, u32[]{:S(2)}, u32[]{:S(2)}) collective-permute-start(bf16[2,3,80,128]{3,2,1,0:T(8,128)(2,1)S(1)} %pad_maximum_fusion.rest_2_), channel_id=1, source_target_pairs={{0,8},{8,0},{16,24},{24,16},{1,9},{9,1},{17,25},{25,17},{2,10},{10... | collective-permute-start | bytes 368648 | tf_op jit(solution)/shard_map/ppermute | solution.py:359
  40.0 8.9 %collective-permute-start.8 = (bf16[2,3,80,128]{3,2,1,0:T(8,128)(2,1)S(1)}, bf16[2,3,80,128]{3,2,1,0:T(8,128)(2,1)S(1)}, u32[]{:S(2)}, u32[]{:S(2)}) collective-permute-start(bf16[2,3,80,128]{3,2,1,0:T(8,128)(2,1)S(1)} %pad_maximum_fusion.rest_2_), channel_id=1, source_target_pairs={{0,16},{8,24},{16,0},{24,8},{1,17},{9,25},{17,1},{25,9},{2,18},{10... | collective-permute-start | bytes 368648 | tf_op jit(solution)/shard_map/ppermute | solution.py:359
  44.4 8.3 %collective-permute-start.14 = (bf16[2,3,80,128]{3,2,1,0:T(8,128)(2,1)S(1)}, bf16[2,3,80,128]{3,2,1,0:T(8,128)(2,1)S(1)}, u32[]{:S(2)}, u32[]{:S(2)}) collective-permute-start(bf16[2,3,80,128]{3,2,1,0:T(8,128)(2,1)S(1)} %pad_maximum_fusion.rest_2_), channel_id=1, source_target_pairs={{0,1},{1,0},{2,3},{3,2},{4,5},{5,4},{6,7},{7,6},{8,9},{9,8},{10,11... | collective-permute-start | bytes 368648 | tf_op jit(solution)/shard_map/ppermute | solution.py:359
  44.9 11.9 %collective-permute-start.27 = (bf16[2,3,80,128]{3,2,1,0:T(8,128)(2,1)S(1)}, bf16[2,3,80,128]{3,2,1,0:T(8,128)(2,1)S(1)}, u32[]{:S(2)}, u32[]{:S(2)}) collective-permute-start(bf16[2,3,80,128]{3,2,1,0:T(8,128)(2,1)S(1)} %pad_maximum_fusion.1.rest_4_), channel_id=1, source_target_pairs={{0,8},{8,0},{16,24},{24,16},{1,9},{9,1},{17,25},{25,17},{2,10},{10... | collective-permute-start | bytes 368648 | tf_op jit(solution)/shard_map/ppermute | solution.py:359
  45.7 7.0 %collective-permute-start.10 = (bf16[1,3,80,128]{3,2,1,0:T(8,128)(2,1)S(1)}, bf16[1,3,80,128]{3,2,1,0:T(8,128)(2,1)S(1)}, u32[]{:S(2)}, u32[]{:S(2)}) collective-permute-start(bf16[1,3,80,128]{3,2,1,0:T(8,128)(2,1)S(1)} %collective-permute-done.7.rest_7_), channel_id=1, source_target_pairs={{0,8},{8,0},{16,24},{24,16},{1,9},{9,1},{17,25},{25,17},{2,10},{10... | collective-permute-start | bytes 184328 | tf_op jit(solution)/shard_map/ppermute | solution.py:359
  47.0 10.4 %collective-permute-start.28 = (bf16[2,3,80,128]{3,2,1,0:T(8,128)(2,1)S(1)}, bf16[2,3,80,128]{3,2,1,0:T(8,128)(2,1)S(1)}, u32[]{:S(2)}, u32[]{:S(2)}) collective-permute-start(bf16[2,3,80,128]{3,2,1,0:T(8,128)(2,1)S(1)} %pad_maximum_fusion.2.rest_5_), channel_id=1, source_target_pairs={{0,8},{8,0},{16,24},{24,16},{1,9},{9,1},{17,25},{25,17},{2,10},{10... | collective-permute-start | bytes 368648 | tf_op jit(solution)/shard_map/ppermute | solution.py:359
  52.7 12.0 %collective-permute-start.29 = (bf16[2,3,80,128]{3,2,1,0:T(8,128)(2,1)S(1)}, bf16[2,3,80,128]{3,2,1,0:T(8,128)(2,1)S(1)}, u32[]{:S(2)}, u32[]{:S(2)}) collective-permute-start(bf16[2,3,80,128]{3,2,1,0:T(8,128)(2,1)S(1)} %pad_maximum_fusion.1.rest_4_), channel_id=1, source_target_pairs={{0,16},{8,24},{16,0},{24,8},{1,17},{9,25},{17,1},{25,9},{2,18},{10... | collective-permute-start | bytes 368648 | tf_op jit(solution)/shard_map/ppermute | solution.py:359
  54.5 12.7 %collective-permute-start.30 = (bf16[2,3,80,128]{3,2,1,0:T(8,128)(2,1)S(1)}, bf16[2,3,80,128]{3,2,1,0:T(8,128)(2,1)S(1)}, u32[]{:S(2)}, u32[]{:S(2)}) collective-permute-start(bf16[2,3,80,128]{3,2,1,0:T(8,128)(2,1)S(1)} %pad_maximum_fusion.2.rest_5_), channel_id=1, source_target_pairs={{0,16},{8,24},{16,0},{24,8},{1,17},{9,25},{17,1},{25,9},{2,18},{10... | collective-permute-start | bytes 368648 | tf_op jit(solution)/shard_map/ppermute | solution.py:359
  56.9 10.4 %collective-permute-start.33 = (bf16[2,3,80,128]{3,2,1,0:T(8,128)(2,1)S(1)}, bf16[2,3,80,128]{3,2,1,0:T(8,128)(2,1)S(1)}, u32[]{:S(2)}, u32[]{:S(2)}) collective-permute-start(bf16[2,3,80,128]{3,2,1,0:T(8,128)(2,1)S(1)} %pad_maximum_fusion.1.rest_4_), channel_id=1, source_target_pairs={{0,1},{1,0},{2,3},{3,2},{4,5},{5,4},{6,7},{7,6},{8,9},{9,8},{10,11... | collective-permute-start | bytes 368648 | tf_op jit(solution)/shard_map/ppermute | solution.py:359
  56.9 11.0 %collective-permute-start.11 = (bf16[2,3,80,128]{3,2,1,0:T(8,128)(2,1)S(1)}, bf16[2,3,80,128]{3,2,1,0:T(8,128)(2,1)S(1)}, u32[]{:S(2)}, u32[]{:S(2)}) collective-permute-start(bf16[2,3,80,128]{3,2,1,0:T(8,128)(2,1)S(1)} %collective-permute-done.8.rest_8_), channel_id=1, source_target_pairs={{0,8},{8,0},{16,24},{24,16},{1,9},{9,1},{17,25},{25,17},{2,10},{10... | collective-permute-start | bytes 368648 | tf_op jit(solution)/shard_map/ppermute | solution.py:359
  57.4 10.4 %collective-permute-start.34 = (bf16[2,3,80,128]{3,2,1,0:T(8,128)(2,1)S(1)}, bf16[2,3,80,128]{3,2,1,0:T(8,128)(2,1)S(1)}, u32[]{:S(2)}, u32[]{:S(2)}) collective-permute-start(bf16[2,3,80,128]{3,2,1,0:T(8,128)(2,1)S(1)} %pad_maximum_fusion.2.rest_5_), channel_id=1, source_target_pairs={{0,1},{1,0},{2,3},{3,2},{4,5},{5,4},{6,7},{7,6},{8,9},{9,8},{10,11... | collective-permute-start | bytes 368648 | tf_op jit(solution)/shard_map/ppermute | solution.py:359
  64.7 6.7 %collective-permute-start.17 = (bf16[2,3,80,128]{3,2,1,0:T(8,128)(2,1)S(1)}, bf16[2,3,80,128]{3,2,1,0:T(8,128)(2,1)S(1)}, u32[]{:S(2)}, u32[]{:S(2)}) collective-permute-start(bf16[2,3,80,128]{3,2,1,0:T(8,128)(2,1)S(1)} %collective-permute-done.5.rest_5_), channel_id=1, source_target_pairs={{0,1},{1,0},{2,3},{3,2},{4,5},{5,4},{6,7},{7,6},{8,9},{9,8},{10,11... | collective-permute-start | bytes 368648 | tf_op jit(solution)/shard_map/ppermute | solution.py:359
  67.3 5.9 %collective-permute-start.31 = (bf16[2,3,80,128]{3,2,1,0:T(8,128)(2,1)S(1)}, bf16[2,3,80,128]{3,2,1,0:T(8,128)(2,1)S(1)}, u32[]{:S(2)}, u32[]{:S(2)}) collective-permute-start(bf16[2,3,80,128]{3,2,1,0:T(8,128)(2,1)S(1)} %collective-permute-done.29.rest_8_), channel_id=1, source_target_pairs={{0,8},{8,0},{16,24},{24,16},{1,9},{9,1},{17,25},{25,17},{2,10},{10... | collective-permute-start | bytes 368648 | tf_op jit(solution)/shard_map/ppermute | solution.py:359
  69.9 21.2 %collective-permute-start.32 = (bf16[2,3,80,128]{3,2,1,0:T(8,128)(2,1)S(1)}, bf16[2,3,80,128]{3,2,1,0:T(8,128)(2,1)S(1)}, u32[]{:S(2)}, u32[]{:S(2)}) collective-permute-start(bf16[2,3,80,128]{3,2,1,0:T(8,128)(2,1)S(1)} %collective-permute-done.30.rest_9_), channel_id=1, source_target_pairs={{0,8},{8,0},{16,24},{24,16},{1,9},{9,1},{17,25},{25,17},{2,10},{10... | collective-permute-start | bytes 368648 | tf_op jit(solution)/shard_map/ppermute | solution.py:359
  71.4 21.0 %collective-permute-start.35 = (bf16[2,3,80,128]{3,2,1,0:T(8,128)(2,1)S(1)}, bf16[2,3,80,128]{3,2,1,0:T(8,128)(2,1)S(1)}, u32[]{:S(2)}, u32[]{:S(2)}) collective-permute-start(bf16[2,3,80,128]{3,2,1,0:T(8,128)(2,1)S(1)} %collective-permute-done.27.rest_6_), channel_id=1, source_target_pairs={{0,1},{1,0},{2,3},{3,2},{4,5},{5,4},{6,7},{7,6},{8,9},{9,8},{10,11... | collective-permute-start | bytes 368648 | tf_op jit(solution)/shard_map/ppermute | solution.py:359
  71.4 21.4 %collective-permute-start.36 = (bf16[2,3,80,128]{3,2,1,0:T(8,128)(2,1)S(1)}, bf16[2,3,80,128]{3,2,1,0:T(8,128)(2,1)}, u32[]{:S(2)}, u32[]{:S(2)}) collective-permute-start(bf16[2,3,80,128]{3,2,1,0:T(8,128)(2,1)S(1)} %collective-permute-done.28.rest_7_), channel_id=1, source_target_pairs={{0,1},{1,0},{2,3},{3,2},{4,5},{5,4},{6,7},{7,6},{8,9},{9,8},{10,11... | collective-permute-start | bytes 368648 | tf_op jit(solution)/shard_map/ppermute | solution.py:359
  73.2 21.5 %collective-permute-start.37 = (bf16[2,3,80,128]{3,2,1,0:T(8,128)(2,1)S(1)}, bf16[2,3,80,128]{3,2,1,0:T(8,128)(2,1)}, u32[]{:S(2)}, u32[]{:S(2)}) collective-permute-start(bf16[2,3,80,128]{3,2,1,0:T(8,128)(2,1)S(1)} %collective-permute-done.29.rest_8_), channel_id=1, source_target_pairs={{0,1},{1,0},{2,3},{3,2},{4,5},{5,4},{6,7},{7,6},{8,9},{9,8},{10,11... | collective-permute-start | bytes 368648 | tf_op jit(solution)/shard_map/ppermute | solution.py:359
  73.2 21.5 %collective-permute-start.38 = (bf16[2,3,80,128]{3,2,1,0:T(8,128)(2,1)S(1)}, bf16[2,3,80,128]{3,2,1,0:T(8,128)(2,1)}, u32[]{:S(2)}, u32[]{:S(2)}) collective-permute-start(bf16[2,3,80,128]{3,2,1,0:T(8,128)(2,1)S(1)} %collective-permute-done.30.rest_9_), channel_id=1, source_target_pairs={{0,1},{1,0},{2,3},{3,2},{4,5},{5,4},{6,7},{7,6},{8,9},{9,8},{10,11... | collective-permute-start | bytes 368648 | tf_op jit(solution)/shard_map/ppermute | solution.py:359
  91.1 7.8 %collective-permute-start.24 = (bf16[768,128]{1,0:T(8,128)(2,1)S(1)}, bf16[768,128]{1,0:T(8,128)(2,1)S(1)}, u32[]{:S(2)}, u32[]{:S(2)}) collective-permute-start(bf16[768,128]{1,0:T(8,128)(2,1)S(1)} %shard_map.94.rest_0_), channel_id=1, source_target_pairs={{0,2},{1,3},{2,0},{3,1},{4,6},{5,7},{6,4},{7,5},{8,10},{9,11},{10,... | collective-permute-start | bytes 589832 | tf_op jit(solution)/shard_map/ppermute | solution.py:359
  92.4 10.8 %collective-permute-start.25 = (bf16[768,128]{1,0:T(8,128)(2,1)S(1)}, bf16[768,128]{1,0:T(8,128)(2,1)S(1)}, u32[]{:S(2)}, u32[]{:S(2)}) collective-permute-start(bf16[768,128]{1,0:T(8,128)(2,1)S(1)} %shard_map.94.rest_0_), channel_id=1, source_target_pairs={{0,4},{1,5},{2,6},{3,7},{4,0},{5,1},{6,2},{7,3},{8,12},{9,13},{10,... | collective-permute-start | bytes 589832 | tf_op jit(solution)/shard_map/ppermute | solution.py:359
  92.8 10.4 %collective-permute-start.26 = (bf16[768,128]{1,0:T(8,128)(2,1)S(1)}, bf16[768,128]{1,0:T(8,128)(2,1)S(1)}, u32[]{:S(2)}, u32[]{:S(2)}) collective-permute-start(bf16[768,128]{1,0:T(8,128)(2,1)S(1)} %shard_map.94.rest_0_), channel_id=1, source_target_pairs={{0,6},{1,7},{2,4},{3,5},{4,2},{5,3},{6,0},{7,1},{8,14},{9,15},{10,... | collective-permute-start | bytes 589832 | tf_op jit(solution)/shard_map/ppermute | solution.py:359
  (47 other events, 473.6 us)

commit v2 on v1

--- a/solution.py
+++ b/solution.py
@@ -13,8 +13,8 @@
 LANES = 128
 
 
-CHUNKS_TWO = ((0,), (1,), (2, 3))
-CHUNKS_ONE = ((0, 1), (2, 3))
+CHUNKS_TWO = ((0, 1), (2, 3))
+CHUNKS_ONE = ((0, 1, 2, 3),)
 
 F32 = jnp.float32
 BF16 = jnp.bfloat16
@@ -94,49 +94,93 @@
     )(*inputs)
 
 
-def pack_filters_kernel(first, second, *outs, plan):
-    chunk = first.shape[2]
-    position = plan.place()[1]
-    for at, taps in enumerate((first, second)):
-        parts = []
-        for block in range(plan.blocks):
-            rows = []
-            for down in range(3):
-                pieces = [
-                    taps[3 * down + side, block * GSIZE : (block + 1) * GSIZE, :].astype(F32)
-                    for side in range(3)
-                ]
-                pieces.append(jnp.zeros((LANES - 3 * GSIZE, chunk), F32))
-                rows.append(jnp.concatenate(pieces, axis=0).T.astype(BF16))
-            parts.append(rows)
-        for step, out in enumerate(outs):
-            wanted = position ^ step
-            for down in range(3):
-                value = parts[0][down]
-                for block in range(1, plan.blocks):
-                    value = jnp.where(wanted == block, parts[block][down], value)
-                out[at, down] = value
-
-
-def pack_fields_kernel(cotangent, hidden, latent, out, *, plan):
-    plane = plan.place()[0]
-    images, width, channels = cotangent.shape
+def pack_kernel(first, second, cotangent, hidden, latent, *rest, plan):
+    outs, sent = rest[: plan.blocks], rest[plan.blocks]
+    taps_held, fields_held, sent_held, semaphores = rest[plan.blocks + 1 :]
+    copies = []
+    for at, source in enumerate((cotangent, hidden, latent)):
+        copies.append(pltpu.make_async_copy(source, fields_held.at[at], semaphores.at[at]))
+    if plan.fast:
+        for at, source in enumerate((first, second)):
+            copies.append(pltpu.make_async_copy(source, taps_held.at[at], semaphores.at[3 + at]))
+    for copy in copies:
+        copy.start()
+    plane, position, _ = plan.place()
+    images, width, channels = plan.images, plan.width, plan.channels
+    own = plan.per_block * GSIZE
     rows = iota((channels, 1), 0)
     lane = iota((1, plan.field_lanes), 1)
-    own = plan.per_block * GSIZE
+    selects = []
     for block in range(plan.blocks):
-        mixed = jnp.zeros((images * width, plan.field_lanes), F32)
-        for at, field in enumerate((hidden, latent)):
+        for at in range(2):
             spans = [
                 (at * own + order * GSIZE, plan.channel(plane, block, order))
                 for order in range(plan.per_block)
             ]
-            select = one_hot(rows, plan.targets(lane, spans))
-            mixed = mixed + dot(field[...].reshape(images * width, channels), select)
+            selects.append(one_hot(rows, plan.targets(lane, spans)))
+    for copy in copies[:3]:
+        copy.wait()
+    for block in range(plan.blocks):
+        mixed = jnp.zeros((images * width, plan.field_lanes), F32)
+        for at in range(2):
+            field = fields_held[1 + at].reshape(images * width, channels)
+            mixed = mixed + dot(field, selects[2 * block + at])
         mixed = mixed.astype(BF16).reshape(images, width, plan.field_lanes)
         for image in range(images):
-            out[block * images + image, :, :channels] = cotangent[image]
-            out[block * images + image, :, channels:] = mixed[image]
+            sent_held[block * images + image, :, :channels] = fields_held[0, image]
+            sent_held[block * images + image, :, channels:] = mixed[image]
+    back = pltpu.make_async_copy(sent_held, sent, semaphores.at[5])
+    back.start()
+    if plan.fast:
+        chunk = first.shape[2]
+        for at in range(2):
+            copies[3 + at].wait()
+            parts = []
+            for block in range(plan.blocks):
+                columns = []
+                for down in range(3):
+                    pieces = [
+                        taps_held[at, 3 * down + side, block * GSIZE : (block + 1) * GSIZE, :].astype(F32)
+                        for side in range(3)
+                    ]
+                    pieces.append(jnp.zeros((LANES - 3 * GSIZE, chunk), F32))
+                    columns.append(jnp.concatenate(pieces, axis=0).T.astype(BF16))
+                parts.append(columns)
+            for turn, out in enumerate(outs):
+                wanted = position ^ turn
+                for down in range(3):
+                    value = parts[0][down]
+                    for block in range(1, plan.blocks):
+                        value = jnp.where(wanted == block, parts[block][down], value)
+                    out[at, down] = value
+    else:
+        for out in outs:
+            out[...] = jnp.zeros(out.shape, BF16)
+    back.wait()
+
+
+def pack(first, second, cotangent, hidden, latent, plan):
+    taps = first.shape
+    piece = (2, 3, taps[2], LANES) if plan.fast else (8, LANES)
+    held = taps if plan.fast else (1, 8, LANES)
+    sent = (plan.height, plan.width, plan.channels + plan.field_lanes)
+    field = (plan.images, plan.width, plan.channels)
+    vmem, anywhere = pl.BlockSpec(memory_space=pltpu.VMEM), pl.BlockSpec(memory_space=pl.ANY)
+    inputs = (first, second, cotangent, hidden, latent)
+    return pl.pallas_call(
+        functools.partial(pack_kernel, plan=plan),
+        out_shape=[pltpu.VMEM(piece, BF16)] * plan.blocks + [jax.ShapeDtypeStruct(sent, BF16)],
+        in_specs=[anywhere] * 5,
+        out_specs=[vmem] * plan.blocks + [anywhere],
+        scratch_shapes=[
+            pltpu.VMEM((2, *held), BF16),
+            pltpu.VMEM((3, *field), BF16),
+            pltpu.VMEM(sent, BF16),
+            pltpu.SemaphoreType.DMA((6,)),
+        ],
+        compiler_params=pltpu.CompilerParams(vmem_limit_bytes=24 * 1024 * 1024),
+        name="pack",
+    )(*(pltpu.with_memory_space_constraint(value, pltpu.HBM) for value in inputs))
 
 
 def group_total(values):
@@ -206,20 +250,18 @@
                 )
 
 
-def load_weights(pieces, weights, plan):
+def load_weights(pieces, weights, orders, plan):
     _, position, core = plan.place()
     for swap, by_order in enumerate(pieces):
-        for order, arrays in enumerate(by_order):
-            step = 0
-            for array in arrays:
+        for at, order in enumerate(orders):
+            turn = 0
+            for array in by_order[order]:
                 for inner in range(array.shape[0]):
                     chunk = array.shape[2]
-                    source = (position ^ step) * plan.images + (core ^ swap)
+                    source = (position ^ turn) * plan.images + (core ^ swap)
                     start = pl.multiple_of(source * chunk, 16)
-                    weights[:, pl.ds(start, chunk), order * LANES : (order + 1) * LANES] = array[
-                        inner
-                    ]
-                    step += 1
+                    weights[:, pl.ds(start, chunk), at * LANES : (at + 1) * LANES] = array[inner]
+                    turn += 1
 
 
 def convolve(padded, weights, width, part):
@@ -256,61 +298,67 @@
     return total.astype(BF16)
 
 
-def block_backward(padded, weights, normed, factor, inverse, plan):
-    grads = []
-    pair = 2 if plan.per_block % 2 == 0 else 1
-    for start in range(0, plan.per_block, pair):
+def block_backward(padded, weights, normed, factor, inverse, orders, plan):
+    grads, start = [], 0
+    while start < len(orders):
+        pair = min(2, len(orders) - start)
         total = convolve(padded, weights, plan.width, slice(start * LANES, (start + pair) * LANES))
         for at in range(pair):
-            part = slice((start + at) * LANES, (start + at + 1) * LANES)
+            order = orders[start + at]
+            part = slice(order * LANES, (order + 1) * LANES)
             incoming = fold_sides(total[:, at * LANES : (at + 1) * LANES], plan.width)
             grads.append(
                 norm_backward(incoming, normed[:, part], factor[:, part], inverse[:, part], plan.number)
             )
+        start += pair
     return grads
 
 
-def hidden_kernel(padded, normed, factor, inverse, *rest, layout, plan):
-    out, weights = rest[layout.total :]
-    layout.fill(rest[: layout.total], weights, plan)
-    grads = block_backward(padded, weights, normed, factor, inverse, plan)
-    rows, half = plan.rows, plan.rows // 2
-    for at, orders in enumerate(plan.mains):
-        out[at * rows : (at + 1) * rows, :] = side_by_side([grads[order] for order in orders])
-    if plan.spare is not None:
-        grad = grads[plan.spare]
-        out[len(plan.mains) * rows :, :] = side_by_side([grad[:half], grad[half:]])
-
-
-def unpack(pieces, main_table, spare_table, rows, plan):
-    total = None
-    for at in range(len(plan.mains)):
-        wide = jnp.concatenate([piece[at * rows : (at + 1) * rows, :] for piece in pieces], axis=1)
-        term = dot(wide, main_table[at])
-        total = term if total is None else total + term
-    halves = [None, None] if total is None else [total[: rows // 2], total[rows // 2 :]]
-    if plan.spare is not None:
-        base = len(plan.mains) * rows
-        wide = jnp.concatenate([piece[base : base + rows // 2, :] for piece in pieces], axis=1)
+def hidden_kernel(padded, normed, factor, inverse, *rest, layout, orders, plan):
+    count = layout.total(orders)
+    out, weights = rest[count:]
+    layout.fill(rest[:count], weights, orders, plan)
+    grads = block_backward(padded, weights, normed, factor, inverse, orders, plan)
+    if len(orders) > 1:
+        out[...] = side_by_side(grads)
+    else:
+        half = plan.rows // 2
+        out[...] = side_by_side([grads[0][:half], grads[0][half:]])
+
+
+def assemble_kernel(*rest, layout, orders, plan):
+    layout.fill(rest[:-1], rest[-1], orders, plan)
+
+
+def unpack(mains, spare, main_table, spare_table, rows):
+    halves = [None, None]
+    for at, pieces in enumerate(mains):
+        term = dot(jnp.concatenate(pieces, axis=1), main_table[at])
+        for half in range(2):
+            part = term[half * (rows // 2) : (half + 1) * (rows // 2)]
+            halves[half] = part if halves[half] is None else halves[half] + part
+    if spare:
+        wide = jnp.concatenate(spare, axis=1)
         for half in range(2):
             term = dot(wide, spare_table[half])
             halves[half] = term if halves[half] is None else halves[half] + term
     return [half.astype(BF16) for half in halves]
 
 
-def latent_kernel(straight, main_table, spare_table, normed, factor, inverse, *rest, layout, plan):
+def latent_kernel(straight, main_table, spare_table, weights, normed, factor, inverse, *rest, plan):
     blocks = plan.blocks
-    pieces = rest[:blocks]
-    out, weights, padded = rest[blocks + layout.total :]
-    layout.fill(rest[blocks : blocks + layout.total], weights, plan)
+    out, padded = rest[-2:]
     width, rows, half = plan.width, plan.rows, plan.rows // 2
     padded[:width, :] = jnp.zeros((width, plan.channels), BF16)
     padded[width + rows :, :] = jnp.zeros((width, plan.channels), BF16)
-    low, high = unpack(pieces, main_table, spare_table, rows, plan)
+    pieces = [[piece[...] for piece in rest[at : at + blocks]] for at in range(0, len(rest) - 2, blocks)]
+    mains, spare = pieces[: len(plan.mains)], pieces[len(plan.mains) :]
+    low, high = unpack(mains, spare[0] if spare else None, main_table, spare_table, rows)
     padded[width : width + half, :] = low
     padded[width + half : width + rows, :] = high
-    grads = block_backward(padded, weights, normed, factor, inverse, plan)
-    for order in range(plan.per_block):
+    orders = list(range(plan.per_block))
+    grads = block_backward(padded, weights, normed, factor, inverse, orders, plan)
+    for order in orders:
         grads[order] = straight[:, order * LANES : (order + 1) * LANES].astype(F32) + grads[order]
     for at, orders in enumerate(plan.mains):
         value = side_by_side([grads[order] for order in orders])
@@ -326,45 +374,49 @@
 
 def spread_kernel(received, main_table, spare_table, out, *, plan):
     position = plan.place()[1]
+    width, base = plan.width, len(plan.mains) * plan.width
     for image in range(plan.images):
         pieces = [
-            received[(position ^ step) * plan.images + image] for step in range(plan.blocks)
+            received[(position ^ turn) * plan.images + image] for turn in range(plan.blocks)
         ]
-        low, high = unpack(pieces, main_table, spare_table, plan.width, plan)
-        out[image, : plan.width // 2, :] = low
-        out[image, plan.width // 2 :, :] = high
+        mains = [
+            [piece[at * width : (at + 1) * width, :] for piece in pieces]
+            for at in range(len(plan.mains))
+        ]
+        spare = [piece[base:, :] for piece in pieces] if plan.spare is not None else None
+        low, high = unpack(mains, spare, main_table, spare_table, width)
+        out[image, : width // 2, :] = low
+        out[image, width // 2 :, :] = high
 
 
 class Layout:
     def __init__(self, pieces):
+        self.pieces = pieces
         self.dynamic = isinstance(pieces, list)
-        if self.dynamic:
-            self.counts = [[len(arrays) for arrays in by_order] for by_order in pieces]
-            self.flat = [array for by_order in pieces for arrays in by_order for array in arrays]
-        else:
-            self.flat = [pieces]
-        self.total = len(self.flat)
-
-    def fill(self, flat, weights, plan):
+
+    def inputs(self, orders):
         if not self.dynamic:
-            weights[...] = flat[0][...]
+            return [self.pieces]
+        return [array for by_order in self.pieces for order in orders for array in by_order[order]]
+
+    def total(self, orders):
+        return len(self.inputs(orders))
+
+    def fill(self, flat, weights, orders, plan):
+        if not self.dynamic:
+            for at, order in enumerate(orders):
+                weights[:, :, at * LANES : (at + 1) * LANES] = flat[0][
+                    :, :, order * LANES : (order + 1) * LANES
+                ]
             return
         flat, nested = list(flat), []
-        for counts in self.counts:
-            nested.append([[flat.pop(0) for _ in range(count)] for count in counts])
-        load_weights(nested, weights, plan)
+        for by_order in self.pieces:
+            nested.append({order: [flat.pop(0) for _ in by_order[order]] for order in orders})
+        load_weights(nested, weights, orders, plan)
 
 
 def flip(array, axis, mask):
     return lax.ppermute(array, axis, [(i, i ^ mask) for i in range(lax.axis_size(axis))])
-
-
-def plane_pieces(filter_two, filter_one, plan):
-    out = [((2, 3, filter_two.shape[2], LANES), BF16)] * plan.blocks
-    mine = call(functools.partial(pack_filters_kernel, plan=plan), out, [filter_two, filter_one])
-    return [mine[0]] + [
-        flip(mine[turn], "rows", turn * plan.images) for turn in range(1, plan.blocks)
-    ]
 
 
 def gathered_filter(mine, chunks):
@@ -397,18 +449,16 @@
     plan = Plan(images, width, channels)
     rows, lanes = plan.rows, plan.lanes
 
+    *packed, sent = pack(filter_two, filter_one, cotangent[:, 0], hidden[:, 0], latent[:, 0], plan)
     if plan.fast:
-        mine = plane_pieces(filter_two, filter_one, plan)
+        mine = [packed[0]] + [
+            flip(packed[turn], "rows", turn * images) for turn in range(1, plan.blocks)
+        ]
         two = Layout(gathered_filter([piece[0] for piece in mine], CHUNKS_TWO))
         one = Layout(gathered_filter([piece[1] for piece in mine], CHUNKS_ONE))
     else:
         two = Layout(assembled_filter(filter_two, plan))
         one = Layout(assembled_filter(filter_one, plan))
-    (sent,) = call(
-        functools.partial(pack_fields_kernel, plan=plan),
-        [((plan.height, width, channels + plan.field_lanes), BF16)],
-        [cotangent[:, 0], hidden[:, 0], latent[:, 0]],
-    )
     received = lax.all_to_all(sent, "rows", 0, 0, tiled=True)
     vectors = jnp.stack([gain_two, shift_two, gain_one, shift_one])
     table = plan.blocks * LANES
@@ -426,23 +476,34 @@
         [received, vectors],
     )
     padded, straight, main_table, spare_table = prepared[:4]
-    weights = pltpu.VMEM((3, channels, lanes), BF16)
-    inputs = [padded, *prepared[4:7], *two.flat]
-    (grad,) = call(
-        functools.partial(hidden_kernel, layout=two, plan=plan),
-        [((plan.packed_rows(rows), LANES), BF16)],
+    parts = plan.mains + ([[plan.spare]] if plan.spare is not None else [])
+    grads = []
+    for orders in parts:
+        inputs = [padded, *prepared[4:7], *two.inputs(orders)]
+        (grad,) = call(
+            functools.partial(hidden_kernel, layout=two, orders=orders, plan=plan),
+            [((rows if len(orders) > 1 else rows // 2, LANES), BF16)],
+            inputs,
+            held=range(len(inputs)),
+            scratch=[pltpu.VMEM((3, channels, len(orders) * LANES), BF16)],
+        )
+        grads.append(grad)
+        grads += [flip(grad, "rows", turn * images) for turn in range(1, plan.blocks)]
+    orders = list(range(plan.per_block))
+    inputs = one.inputs(orders)
+    (weights,) = call(
+        functools.partial(assemble_kernel, layout=one, orders=orders, plan=plan),
+        [((3, channels, lanes), BF16)],
         inputs,
         held=range(len(inputs)),
-        scratch=[weights],
     )
-    grads = [grad] + [flip(grad, "rows", turn * images) for turn in range(1, plan.blocks)]
-    inputs = [straight, main_table, spare_table, *prepared[7:10], *grads, *one.flat]
+    inputs = [straight, main_table, spare_table, weights, *prepared[7:10], *grads]
     (result,) = call(
-        functools.partial(latent_kernel, layout=one, plan=plan),
+        functools.partial(latent_kernel, plan=plan),
         [((plan.height, plan.packed_rows(width), LANES), BF16)],
         inputs,
         held=range(len(inputs)),
-        scratch=[weights, pltpu.VMEM((rows + 2 * width, channels), BF16)],
+        scratch=[pltpu.VMEM((rows + 2 * width, channels), BF16)],
     )
     result = lax.all_to_all(result, "rows", 0, 0, tiled=True)
     (out,) = call(

time: 119 us -> 93.2 us (0.78)
  waiting for transfers between devices: 41.9 us -> 27.8 us
  local copies, waits for them, and re-layouts: 18.9 us -> 10.2 us
  starting transfers between devices: 34.1 us -> 29 us
  Pallas kernels: 14.1 us -> 15.7 us
    ppermute x41 -> x30, waiting for transfers between devices: 41.9 us -> 27.8 us  [flip(): lax.ppermute(array, axis, [(i, i ^ mask) for i in range(lax.axis_size(axi...]
    unnamed x74 -> x48, local copies, waits for them, and re-layouts: 18.8 us -> 10.2 us
    ppermute x41 -> x30, starting transfers between devices: 30.4 us -> 24.7 us  [flip(): lax.ppermute(array, axis, [(i, i ^ mask) for i in range(lax.axis_size(axi...]
    pallas_call x0 -> x1, Pallas kernels: none -> 3.08 us  [pack(): pl.pallas_call(functools.partial(pack_kernel, plan=plan), out_shape=[pltp...]
    pallas_call x6, Pallas kernels: 14.1 us -> 12.6 us  [call(): pl.pallas_call(body, out_shape=outs, in_specs=[vmem] * len(inputs), out_s...]
  transfers between devices with their start and end apart: 42 -> 31, of which waited for: 14 -> 9; matrix products, arithmetic and copies ran while one was open for 0% -> 0% of each run, Pallas kernels for 7% -> 8%
where the time goes in v2:
time: 93.2 us; the launch traced here: 92.9 us
  starting transfers between devices  29 us (31%)
  waiting for transfers between devices  27.8 us (30%)
  Pallas kernels  15.7 us (17%)
  local copies, waits for them, and re-layouts  10.2 us (11%)
  blocking collectives  9.75 us (10%)
    ppermute x30, waiting for transfers between devices, flip(): lax.ppermute(array, axis, [(i, i ^ mask) for i in range(lax.axis_size(axi...  27.8 us
    ppermute x30, starting transfers between devices, flip(): lax.ppermute(array, axis, [(i, i ^ mask) for i in range(lax.axis_size(axi...  24.7 us
    pallas_call x6, Pallas kernels, call(): pl.pallas_call(body, out_shape=outs, in_specs=[vmem] * len(inputs), out_s...  12.6 us
    unnamed x48, local copies, waits for them, and re-layouts  10.2 us
    all_to_all x1, blocking collectives, step(): result = lax.all_to_all(result, 'rows', 0, 0, tiled=True)  9.75 us
    all_to_all x1, starting transfers between devices, step(): received = lax.all_to_all(sent, 'rows', 0, 0, tiled=True)  4.3 us
    pallas_call x1, Pallas kernels, pack(): pl.pallas_call(functools.partial(pack_kernel, plan=plan), out_shape=[pltp...  3.08 us
  transfers between devices with their start and end apart: 31, of which 9 were waited for; matrix products, arithmetic and copies ran while one was open for 0% of the time, Pallas kernels for 8%

profile of v2, /device:TPU:0, one launch (start us, length us, event | category | flops | bytes accessed | tf_op | source)
XLA Modules:
  0.0 92.9 jit_solution(8120865145294777618)
XLA Ops:
  0.0 3.1 %pack.1 = (bf16[2,3,80,128]{3,2,1,0:T(8,128)(2,1)S(1)}, bf16[2,3,80,128]{3,2,1,0:T(8,128)(2,1)S(1)}, bf16[2,3,80,128]{3,2,1,0:T(8,128)(2,1)S(1)}, bf16[2,3,80,12...) custom-call(bf16[9,160,80]{2,1,0:T(8,128)(2,1)} %first.1, bf16[9,160,80]{2,1,0:T(8,128)(2,1)} %second.1, ...), custom_call_target="tpu_custom_call" | custom-call | tf_op jit(solution)/shard_map/pack/pallas_call | solution.py:170
  3.1 3.1 %collective-permute-start.1 = (bf16[2,3,80,128]{3,2,1,0:T(8,128)(2,1)S(1)}, bf16[2,3,80,128]{3,2,1,0:T(8,128)(2,1)S(1)}, u32[]{:S(2)}, u32[]{:S(2)}) collective-permute-start(bf16[2,3,80,128]{3,2,1,0:T(8,128)(2,1)S(1)} %get-tuple-element.26), channel_id=1, source_target_pairs={{0,4},{1,5},{2,6},{3,7},{4,0},{5,1},{6,2},{7,3},{8,12},{9,13},{10,... | collective-permute-start | bytes 368648 | tf_op jit(solution)/shard_map/ppermute | solution.py:419
  6.1 1.4 %collective-permute-start.2 = (bf16[2,3,80,128]{3,2,1,0:T(8,128)(2,1)S(1)}, bf16[2,3,80,128]{3,2,1,0:T(8,128)(2,1)S(1)}, u32[]{:S(2)}, u32[]{:S(2)}) collective-permute-start(bf16[2,3,80,128]{3,2,1,0:T(8,128)(2,1)S(1)} %get-tuple-element.27), channel_id=1, source_target_pairs={{0,6},{1,7},{2,4},{3,5},{4,2},{5,3},{6,0},{7,1},{8,14},{9,15},{10,... | collective-permute-start | bytes 368648 | tf_op jit(solution)/shard_map/ppermute | solution.py:419
  7.7 4.3 %all-to-all-start = ((bf16[8,64,1024]{2,1,0:T(8,128)(2,1)}), bf16[8,64,1024]{2,1,0:T(8,128)(2,1)S(1)}, u32[]{:S(2)}, u32[]{:S(2)}) async-start(bf16[8,64,1024]{2,1,0:T(8,128)(2,1)} %get-tuple-element.20), calls=%async_computation | async-start | bytes 2097152 | tf_op jit(solution)/shard_map/all_to_all | solution.py:462
  12.0 1.2 %collective-permute-done.2 = bf16[2,3,80,128]{3,2,1,0:T(8,128)(2,1)S(1)} collective-permute-done((bf16[2,3,80,128]{3,2,1,0:T(8,128)(2,1)S(1)}, bf16[2,3,80,128]{3,2,1,0:T(8,128)(2,1)S(1)}, u32[]{:S(2)}, u32[]{:S(2)}) %collective-permute-start.2) | collective-permute-done | bytes 122912 | tf_op jit(solution)/shard_map/ppermute | solution.py:419
  13.2 2.7 %collective-permute-start.13 = (bf16[2,3,80,128]{3,2,1,0:T(8,128)(2,1)S(1)}, bf16[2,3,80,128]{3,2,1,0:T(8,128)(2,1)S(1)}, u32[]{:S(2)}, u32[]{:S(2)}) collective-permute-start(bf16[2,3,80,128]{3,2,1,0:T(8,128)(2,1)S(1)} %pad_maximum_fusion.2.rest_1_), channel_id=1, source_target_pairs={{0,16},{8,24},{16,0},{24,8},{1,17},{9,25},{17,1},{25,9},{2,18},{10... | collective-permute-start | bytes 368648 | tf_op jit(solution)/shard_map/ppermute | solution.py:419
  16.4 2.7 %collective-permute-start.4 = (bf16[4,3,80,128]{3,2,1,0:T(8,128)(2,1)S(1)}, bf16[4,3,80,128]{3,2,1,0:T(8,128)(2,1)S(1)}, u32[]{:S(2)}, u32[]{:S(2)}) collective-permute-start(bf16[4,3,80,128]{3,2,1,0:T(8,128)(2,1)S(1)} %pad_maximum_fusion.rest_0_), channel_id=1, source_target_pairs={{0,16},{8,24},{16,0},{24,8},{1,17},{9,25},{17,1},{25,9},{2,18},{10... | collective-permute-start | bytes 737288 | tf_op jit(solution)/shard_map/ppermute | solution.py:419
  19.0 1.6 %collective-permute-start.11 = (bf16[2,3,80,128]{3,2,1,0:T(8,128)(2,1)S(1)}, bf16[2,3,80,128]{3,2,1,0:T(8,128)(2,1)S(1)}, u32[]{:S(2)}, u32[]{:S(2)}) collective-permute-start(bf16[2,3,80,128]{3,2,1,0:T(8,128)(2,1)S(1)} %pad_maximum_fusion.2.rest_1_), channel_id=1, source_target_pairs={{0,8},{8,0},{16,24},{24,16},{1,9},{9,1},{17,25},{25,17},{2,10},{10... | collective-permute-start | bytes 368648 | tf_op jit(solution)/shard_map/ppermute | solution.py:419
  21.0 9.4 %collective-permute-done.13.rest_5_ = bf16[2,3,80,128]{3,2,1,0:T(8,128)(2,1)S(1)} collective-permute-done((bf16[2,3,80,128]{3,2,1,0:T(8,128)(2,1)S(1)}, bf16[2,3,80,128]{3,2,1,0:T(8,128)(2,1)S(1)}, u32[]{:S(2)}, u32[]{:S(2)}) %collective-permute-start.13) | collective-permute-done | bytes 122912 | tf_op jit(solution)/shard_map/ppermute | solution.py:419
  30.4 2.6 %collective-permute-done.12.rest_4_ = bf16[2,3,80,128]{3,2,1,0:T(8,128)(2,1)S(1)} collective-permute-done((bf16[2,3,80,128]{3,2,1,0:T(8,128)(2,1)S(1)}, bf16[2,3,80,128]{3,2,1,0:T(8,128)(2,1)S(1)}, u32[]{:S(2)}, u32[]{:S(2)}) %collective-permute-start.12) | collective-permute-done | bytes 122912 | tf_op jit(solution)/shard_map/ppermute | solution.py:419
  33.1 2.0 %collective-permute-start.23 = (bf16[2,3,80,128]{3,2,1,0:T(8,128)(2,1)S(1)}, bf16[2,3,80,128]{3,2,1,0:T(8,128)(2,1)S(1)}, u32[]{:S(2)}, u32[]{:S(2)}) collective-permute-start(bf16[2,3,80,128]{3,2,1,0:T(8,128)(2,1)S(1)} %collective-permute-done.12.rest_4_), channel_id=1, source_target_pairs={{0,8},{8,0},{16,24},{24,16},{1,9},{9,1},{17,25},{25,17},{2,10},{10... | collective-permute-start | bytes 368648 | tf_op jit(solution)/shard_map/ppermute | solution.py:419
  35.8 0.7 copy-done.4
  36.5 0.8 collective-permute-done.4.rest_2_
  37.3 1.1 %collective-permute-start.5 = (bf16[4,3,80,128]{3,2,1,0:T(8,128)(2,1)S(1)}, bf16[4,3,80,128]{3,2,1,0:T(8,128)(2,1)S(1)}, u32[]{:S(2)}, u32[]{:S(2)}) collective-permute-start(bf16[4,3,80,128]{3,2,1,0:T(8,128)(2,1)S(1)} %collective-permute-done.4.rest_2_), channel_id=1, source_target_pairs={{0,8},{8,0},{16,24},{24,16},{1,9},{9,1},{17,25},{25,17},{2,10},{10... | collective-permute-start | bytes 737288 | tf_op jit(solution)/shard_map/ppermute | solution.py:419
  38.4 1.5 %collective-permute-done.24.rest_1_ = bf16[2,3,80,128]{3,2,1,0:T(8,128)(2,1)S(1)} collective-permute-done((bf16[2,3,80,128]{3,2,1,0:T(8,128)(2,1)S(1)}, bf16[2,3,80,128]{3,2,1,0:T(8,128)(2,1)S(1)}, u32[]{:S(2)}, u32[]{:S(2)}) %collective-permute-start.24) | collective-permute-done | bytes 122912 | tf_op jit(solution)/shard_map/ppermute | solution.py:419
  39.9 2.6 %collective-permute-done.23.rest_0_ = bf16[2,3,80,128]{3,2,1,0:T(8,128)(2,1)S(1)} collective-permute-done((bf16[2,3,80,128]{3,2,1,0:T(8,128)(2,1)S(1)}, bf16[2,3,80,128]{3,2,1,0:T(8,128)(2,1)S(1)}, u32[]{:S(2)}, u32[]{:S(2)}) %collective-permute-start.23) | collective-permute-done | bytes 122912 | tf_op jit(solution)/shard_map/ppermute | solution.py:419
  48.9 4.1 %collective-permute-done.5.rest_3_ = bf16[4,3,80,128]{3,2,1,0:T(8,128)(2,1)S(1)} collective-permute-done((bf16[4,3,80,128]{3,2,1,0:T(8,128)(2,1)S(1)}, bf16[4,3,80,128]{3,2,1,0:T(8,128)(2,1)S(1)}, u32[]{:S(2)}, u32[]{:S(2)}) %collective-permute-start.5) | collective-permute-done | bytes 245792 | tf_op jit(solution)/shard_map/ppermute | solution.py:419
  54.3 3.1 %shard_map.91 = (bf16[640,640]{1,0:T(8,128)(2,1)S(1)}, bf16[512,512]{1,0:T(8,128)(2,1)S(1)}, bf16[1,512,640]{2,1,0:T(8,128)(2,1)S(1)}, bf16[2,512,640]{2,1,0:T(8...) custom-call(bf16[8,64,1024]{2,1,0:T(8,128)(2,1)S(1)} %all-to-all-don, ...), custom_call_target="tpu_custom_call" | custom-call | tf_op jit(solution)/shard_map/pallas_call | solution.py:87
  57.4 0.9 %copy-done.7 = bf16[2,3,80,128]{3,2,1,0:T(8,128)(2,1)S(1)} copy-done((bf16[2,3,80,128]{3,2,1,0:T(8,128)(2,1)S(1)}, bf16[2,3,80,128]{3,2,1,0:T(8,128)(2,1)}, u32[]{:S(2)}) %copy-start.7) | copy-done | bytes 122904
  58.4 0.9 copy-done.11
  59.3 0.9 copy-done.17
  60.2 0.9 copy-done.19
  61.1 1.1 %shard_map.94.rest_4_ = bf16[256,128]{1,0:T(8,128)(2,1)S(1)} custom-call(bf16[640,640]{1,0:T(8,128)(2,1)S(1)} %get-tuple-element.31.padded, f32[512,512]{1,0:T(8,128)S(1)} %get-tuple-element.32.normed, f32[512,512]{1,0:T(8,128)S(1)} %get-tuple-element.33.factor, f32[1,512]{1,0:T(1,128)S(1)} %get-tuple-element.34.inverse, ...), custom_call_target="tpu_custom_call" | custom-call | tf_op jit(solution)/shard_map/pallas_call | solution.py:87
  62.1 1.7 %collective-permute-start.27 = (bf16[256,128]{1,0:T(8,128)(2,1)S(1)}, bf16[256,128]{1,0:T(8,128)(2,1)S(1)}, u32[]{:S(2)}, u32[]{:S(2)}) collective-permute-start(bf16[256,128]{1,0:T(8,128)(2,1)S(1)} %shard_map.94.rest_4_), channel_id=1, source_target_pairs={{0,2},{1,3},{2,0},{3,1},{4,6},{5,7},{6,4},{7,5},{8,10},{9,11},{10,... | collective-permute-start | bytes 196616 | tf_op jit(solution)/shard_map/ppermute | solution.py:419
  63.9 3.3 %shard_map.93.rest_0_ = bf16[512,128]{1,0:T(8,128)(2,1)S(1)} custom-call(bf16[640,640]{1,0:T(8,128)(2,1)S(1)} %get-tuple-element.31.padded, f32[512,512]{1,0:T(8,128)S(1)} %get-tuple-element.32.normed, f32[512,512]{1,0:T(8,128)S(1)} %get-tuple-element.33.factor, f32[1,512]{1,0:T(1,128)S(1)} %get-tuple-element.34.inverse, ...), custom_call_target="tpu_custom_call" | custom-call | tf_op jit(solution)/shard_map/pallas_call | solution.py:87
  67.7 1.6 %collective-permute-start.21 = (bf16[512,128]{1,0:T(8,128)(2,1)S(1)}, bf16[512,128]{1,0:T(8,128)(2,1)S(1)}, u32[]{:S(2)}, u32[]{:S(2)}) collective-permute-start(bf16[512,128]{1,0:T(8,128)(2,1)S(1)} %shard_map.93.rest_0_), channel_id=1, source_target_pairs={{0,4},{1,5},{2,6},{3,7},{4,0},{5,1},{6,2},{7,3},{8,12},{9,13},{10,... | collective-permute-start | bytes 393224 | tf_op jit(solution)/shard_map/ppermute | solution.py:419
  69.3 1.5 %collective-permute-start.22 = (bf16[512,128]{1,0:T(8,128)(2,1)S(1)}, bf16[512,128]{1,0:T(8,128)(2,1)S(1)}, u32[]{:S(2)}, u32[]{:S(2)}) collective-permute-start(bf16[512,128]{1,0:T(8,128)(2,1)S(1)} %shard_map.93.rest_0_), channel_id=1, source_target_pairs={{0,6},{1,7},{2,4},{3,5},{4,2},{5,3},{6,0},{7,1},{8,14},{9,15},{10,... | collective-permute-start | bytes 393224 | tf_op jit(solution)/shard_map/ppermute | solution.py:419
  70.8 1.5 %collective-permute-start.28 = (bf16[256,128]{1,0:T(8,128)(2,1)S(1)}, bf16[256,128]{1,0:T(8,128)(2,1)S(1)}, u32[]{:S(2)}, u32[]{:S(2)}) collective-permute-start(bf16[256,128]{1,0:T(8,128)(2,1)S(1)} %shard_map.94.rest_4_), channel_id=1, source_target_pairs={{0,4},{1,5},{2,6},{3,7},{4,0},{5,1},{6,2},{7,3},{8,12},{9,13},{10,... | collective-permute-start | bytes 196616 | tf_op jit(solution)/shard_map/ppermute | solution.py:419
  73.0 5.3 %collective-permute-done.28.rest_6_ = bf16[256,128]{1,0:T(8,128)(2,1)S(1)} collective-permute-done((bf16[256,128]{1,0:T(8,128)(2,1)S(1)}, bf16[256,128]{1,0:T(8,128)(2,1)S(1)}, u32[]{:S(2)}, u32[]{:S(2)}) %collective-permute-start.28) | collective-permute-done | bytes 65568 | tf_op jit(solution)/shard_map/ppermute | solution.py:419
  78.3 3.4 %shard_map.95 = bf16[8,96,128]{2,1,0:T(8,128)(2,1)S(1)} custom-call(bf16[512,512]{1,0:T(8,128)(2,1)S(1)} %get-tuple-element.21.straight, bf16[1,512,640]{2,1,0:T(8,128)(2,1)S(1)} %get-tuple-element.22.main_table, bf16[2,512,640]{2,1,0:T(8,128)(2,1)S(1)} %get-tuple-element.23.spare_table, bf16[3,640,512]{2,1,0:T(8,128)(2,1)S(1)} %shard_map.92.weights, ...), custom_call_target="tpu_custom_call" | custom-call | tf_op jit(solution)/shard_map/pallas_call | solution.py:87
  81.6 9.7 %all_to_all.10.received = bf16[8,96,128]{2,1,0:T(8,128)(2,1)S(1)} all-to-all(bf16[8,96,128]{2,1,0:T(8,128)(2,1)S(1)} %shard_map.95), channel_id=1, replica_groups=mesh['dp'=4,'rows'=8] {'rows'}, dimensions={0} | all-to-all | bytes 393216 | tf_op jit(solution)/shard_map/all_to_all | solution.py:508
  91.4 1.5 %shard_map.96 = bf16[2,64,640]{2,1,0:T(8,128)(2,1)} custom-call(bf16[8,96,128]{2,1,0:T(8,128)(2,1)S(1)} %all_to_all.10.received, bf16[1,512,640]{2,1,0:T(8,128)(2,1)S(1)} %get-tuple-element.22.main_table, bf16[2,512,640]{2,1,0:T(8,128)(2,1)S(1)} %get-tuple-element.23.spare_table), custom_call_target="tpu_custom_call" | custom-call | tf_op jit(solution)/shard_map/pallas_call | solution.py:87
  (98 shorter events, 10.7 us)
Async XLA Ops:
  3.1 8.9 %collective-permute-start.1 = (bf16[2,3,80,128]{3,2,1,0:T(8,128)(2,1)S(1)}, bf16[2,3,80,128]{3,2,1,0:T(8,128)(2,1)S(1)}, u32[]{:S(2)}, u32[]{:S(2)}) collective-permute-start(bf16[2,3,80,128]{3,2,1,0:T(8,128)(2,1)S(1)} %get-tuple-element.26), channel_id=1, source_target_pairs={{0,4},{1,5},{2,6},{3,7},{4,0},{5,1},{6,2},{7,3},{8,12},{9,13},{10,... | collective-permute-start | bytes 368648 | tf_op jit(solution)/shard_map/ppermute | solution.py:419
  6.1 7.0 %collective-permute-start.2 = (bf16[2,3,80,128]{3,2,1,0:T(8,128)(2,1)S(1)}, bf16[2,3,80,128]{3,2,1,0:T(8,128)(2,1)S(1)}, u32[]{:S(2)}, u32[]{:S(2)}) collective-permute-start(bf16[2,3,80,128]{3,2,1,0:T(8,128)(2,1)S(1)} %get-tuple-element.27), channel_id=1, source_target_pairs={{0,6},{1,7},{2,4},{3,5},{4,2},{5,3},{6,0},{7,1},{8,14},{9,15},{10,... | collective-permute-start | bytes 368648 | tf_op jit(solution)/shard_map/ppermute | solution.py:419
  7.6 8.3 %collective-permute-start = (bf16[2,3,80,128]{3,2,1,0:T(8,128)(2,1)S(1)}, bf16[2,3,80,128]{3,2,1,0:T(8,128)(2,1)S(1)}, u32[]{:S(2)}, u32[]{:S(2)}) collective-permute-start(bf16[2,3,80,128]{3,2,1,0:T(8,128)(2,1)S(1)} %get-tuple-element.25), channel_id=1, source_target_pairs={{0,2},{1,3},{2,0},{3,1},{4,6},{5,7},{6,4},{7,5},{8,10},{9,11},{10,... | collective-permute-start | bytes 368648 | tf_op jit(solution)/shard_map/ppermute | solution.py:419
  7.7 46.5 %copy-start.23 = (f32[640]{0:T(1024)S(1)}, f32[640]{0:T(1024)}, u32[]{:S(2)}) copy-start(f32[640]{0:T(1024)} %param.15) | copy-start | bytes 7684
  7.7 46.6 %all-to-all-start = ((bf16[8,64,1024]{2,1,0:T(8,128)(2,1)}), bf16[8,64,1024]{2,1,0:T(8,128)(2,1)S(1)}, u32[]{:S(2)}, u32[]{:S(2)}) async-start(bf16[8,64,1024]{2,1,0:T(8,128)(2,1)} %get-tuple-element.20), calls=%async_computation | async-start | bytes 2097152 | tf_op jit(solution)/shard_map/all_to_all | solution.py:462
  13.2 17.2 %collective-permute-start.13 = (bf16[2,3,80,128]{3,2,1,0:T(8,128)(2,1)S(1)}, bf16[2,3,80,128]{3,2,1,0:T(8,128)(2,1)S(1)}, u32[]{:S(2)}, u32[]{:S(2)}) collective-permute-start(bf16[2,3,80,128]{3,2,1,0:T(8,128)(2,1)S(1)} %pad_maximum_fusion.2.rest_1_), channel_id=1, source_target_pairs={{0,16},{8,24},{16,0},{24,8},{1,17},{9,25},{17,1},{25,9},{2,18},{10... | collective-permute-start | bytes 368648 | tf_op jit(solution)/shard_map/ppermute | solution.py:419
  15.9 17.1 %collective-permute-start.12 = (bf16[2,3,80,128]{3,2,1,0:T(8,128)(2,1)S(1)}, bf16[2,3,80,128]{3,2,1,0:T(8,128)(2,1)S(1)}, u32[]{:S(2)}, u32[]{:S(2)}) collective-permute-start(bf16[2,3,80,128]{3,2,1,0:T(8,128)(2,1)S(1)} %pad_maximum_fusion.1.rest_0_), channel_id=1, source_target_pairs={{0,16},{8,24},{16,0},{24,8},{1,17},{9,25},{17,1},{25,9},{2,18},{10... | collective-permute-start | bytes 368648 | tf_op jit(solution)/shard_map/ppermute | solution.py:419
  16.4 21.0 %collective-permute-start.4 = (bf16[4,3,80,128]{3,2,1,0:T(8,128)(2,1)S(1)}, bf16[4,3,80,128]{3,2,1,0:T(8,128)(2,1)S(1)}, u32[]{:S(2)}, u32[]{:S(2)}) collective-permute-start(bf16[4,3,80,128]{3,2,1,0:T(8,128)(2,1)S(1)} %pad_maximum_fusion.rest_0_), channel_id=1, source_target_pairs={{0,16},{8,24},{16,0},{24,8},{1,17},{9,25},{17,1},{25,9},{2,18},{10... | collective-permute-start | bytes 737288 | tf_op jit(solution)/shard_map/ppermute | solution.py:419
  19.0 14.1 %collective-permute-start.11 = (bf16[2,3,80,128]{3,2,1,0:T(8,128)(2,1)S(1)}, bf16[2,3,80,128]{3,2,1,0:T(8,128)(2,1)S(1)}, u32[]{:S(2)}, u32[]{:S(2)}) collective-permute-start(bf16[2,3,80,128]{3,2,1,0:T(8,128)(2,1)S(1)} %pad_maximum_fusion.2.rest_1_), channel_id=1, source_target_pairs={{0,8},{8,0},{16,24},{24,16},{1,9},{9,1},{17,25},{25,17},{2,10},{10... | collective-permute-start | bytes 368648 | tf_op jit(solution)/shard_map/ppermute | solution.py:419
  20.6 12.5 %collective-permute-start.10 = (bf16[2,3,80,128]{3,2,1,0:T(8,128)(2,1)S(1)}, bf16[2,3,80,128]{3,2,1,0:T(8,128)(2,1)}, u32[]{:S(2)}, u32[]{:S(2)}) collective-permute-start(bf16[2,3,80,128]{3,2,1,0:T(8,128)(2,1)S(1)} %pad_maximum_fusion.1.rest_0_), channel_id=1, source_target_pairs={{0,8},{8,0},{16,24},{24,16},{1,9},{9,1},{17,25},{25,17},{2,10},{10... | collective-permute-start | bytes 368648 | tf_op jit(solution)/shard_map/ppermute | solution.py:419
  30.4 4.7 %collective-permute-start.15 = (bf16[2,3,80,128]{3,2,1,0:T(8,128)(2,1)S(1)}, bf16[2,3,80,128]{3,2,1,0:T(8,128)(2,1)S(1)}, u32[]{:S(2)}, u32[]{:S(2)}) collective-permute-start(bf16[2,3,80,128]{3,2,1,0:T(8,128)(2,1)S(1)} %pad_maximum_fusion.2.rest_1_), channel_id=1, source_target_pairs={{0,1},{1,0},{2,3},{3,2},{4,5},{5,4},{6,7},{7,6},{8,9},{9,8},{10,11... | collective-permute-start | bytes 368648 | tf_op jit(solution)/shard_map/ppermute | solution.py:419
  33.1 2.8 %collective-permute-start.14 = (bf16[2,3,80,128]{3,2,1,0:T(8,128)(2,1)S(1)}, bf16[2,3,80,128]{3,2,1,0:T(8,128)(2,1)S(1)}, u32[]{:S(2)}, u32[]{:S(2)}) collective-permute-start(bf16[2,3,80,128]{3,2,1,0:T(8,128)(2,1)S(1)} %pad_maximum_fusion.1.rest_0_), channel_id=1, source_target_pairs={{0,1},{1,0},{2,3},{3,2},{4,5},{5,4},{6,7},{7,6},{8,9},{9,8},{10,11... | collective-permute-start | bytes 368648 | tf_op jit(solution)/shard_map/ppermute | solution.py:419
  33.1 6.8 %collective-permute-start.24 = (bf16[2,3,80,128]{3,2,1,0:T(8,128)(2,1)S(1)}, bf16[2,3,80,128]{3,2,1,0:T(8,128)(2,1)S(1)}, u32[]{:S(2)}, u32[]{:S(2)}) collective-permute-start(bf16[2,3,80,128]{3,2,1,0:T(8,128)(2,1)S(1)} %collective-permute-done.13.rest_5_), channel_id=1, source_target_pairs={{0,8},{8,0},{16,24},{24,16},{1,9},{9,1},{17,25},{25,17},{2,10},{10... | collective-permute-start | bytes 368648 | tf_op jit(solution)/shard_map/ppermute | solution.py:419
  33.1 9.4 %collective-permute-start.23 = (bf16[2,3,80,128]{3,2,1,0:T(8,128)(2,1)S(1)}, bf16[2,3,80,128]{3,2,1,0:T(8,128)(2,1)S(1)}, u32[]{:S(2)}, u32[]{:S(2)}) collective-permute-start(bf16[2,3,80,128]{3,2,1,0:T(8,128)(2,1)S(1)} %collective-permute-done.12.rest_4_), channel_id=1, source_target_pairs={{0,8},{8,0},{16,24},{24,16},{1,9},{9,1},{17,25},{25,17},{2,10},{10... | collective-permute-start | bytes 368648 | tf_op jit(solution)/shard_map/ppermute | solution.py:419
  35.7 12.0 %collective-permute-start.3 = (bf16[4,3,80,128]{3,2,1,0:T(8,128)(2,1)S(1)}, bf16[4,3,80,128]{3,2,1,0:T(8,128)(2,1)S(1)}, u32[]{:S(2)}, u32[]{:S(2)}) collective-permute-start(bf16[4,3,80,128]{3,2,1,0:T(8,128)(2,1)S(1)} %pad_maximum_fusion.rest_0_), channel_id=1, source_target_pairs={{0,8},{8,0},{16,24},{24,16},{1,9},{9,1},{17,25},{25,17},{2,10},{10... | collective-permute-start | bytes 737288 | tf_op jit(solution)/shard_map/ppermute | solution.py:419
  36.5 6.7 %collective-permute-start.19 = (bf16[2,3,80,128]{3,2,1,0:T(8,128)(2,1)S(1)}, bf16[2,3,80,128]{3,2,1,0:T(8,128)(2,1)S(1)}, u32[]{:S(2)}, u32[]{:S(2)}) collective-permute-start(bf16[2,3,80,128]{3,2,1,0:T(8,128)(2,1)S(1)} %collective-permute-done.13.rest_5_), channel_id=1, source_target_pairs={{0,1},{1,0},{2,3},{3,2},{4,5},{5,4},{6,7},{7,6},{8,9},{9,8},{10,11... | collective-permute-start | bytes 368648 | tf_op jit(solution)/shard_map/ppermute | solution.py:419
  37.3 15.7 %collective-permute-start.5 = (bf16[4,3,80,128]{3,2,1,0:T(8,128)(2,1)S(1)}, bf16[4,3,80,128]{3,2,1,0:T(8,128)(2,1)S(1)}, u32[]{:S(2)}, u32[]{:S(2)}) collective-permute-start(bf16[4,3,80,128]{3,2,1,0:T(8,128)(2,1)S(1)} %collective-permute-done.4.rest_2_), channel_id=1, source_target_pairs={{0,8},{8,0},{16,24},{24,16},{1,9},{9,1},{17,25},{25,17},{2,10},{10... | collective-permute-start | bytes 737288 | tf_op jit(solution)/shard_map/ppermute | solution.py:419
  39.9 5.1 %collective-permute-start.18 = (bf16[2,3,80,128]{3,2,1,0:T(8,128)(2,1)S(1)}, bf16[2,3,80,128]{3,2,1,0:T(8,128)(2,1)S(1)}, u32[]{:S(2)}, u32[]{:S(2)}) collective-permute-start(bf16[2,3,80,128]{3,2,1,0:T(8,128)(2,1)S(1)} %collective-permute-done.12.rest_4_), channel_id=1, source_target_pairs={{0,1},{1,0},{2,3},{3,2},{4,5},{5,4},{6,7},{7,6},{8,9},{9,8},{10,11... | collective-permute-start | bytes 368648 | tf_op jit(solution)/shard_map/ppermute | solution.py:419
  42.5 3.8 %collective-permute-start.17 = (bf16[2,3,80,128]{3,2,1,0:T(8,128)(2,1)S(1)}, bf16[2,3,80,128]{3,2,1,0:T(8,128)(2,1)S(1)}, u32[]{:S(2)}, u32[]{:S(2)}) collective-permute-start(bf16[2,3,80,128]{3,2,1,0:T(8,128)(2,1)S(1)} %collective-permute-done.11.rest_3_), channel_id=1, source_target_pairs={{0,1},{1,0},{2,3},{3,2},{4,5},{5,4},{6,7},{7,6},{8,9},{9,8},{10,11... | collective-permute-start | bytes 368648 | tf_op jit(solution)/shard_map/ppermute | solution.py:419
  43.8 4.0 %collective-permute-start.26 = (bf16[2,3,80,128]{3,2,1,0:T(8,128)(2,1)S(1)}, bf16[2,3,80,128]{3,2,1,0:T(8,128)(2,1)S(1)}, u32[]{:S(2)}, u32[]{:S(2)}) collective-permute-start(bf16[2,3,80,128]{3,2,1,0:T(8,128)(2,1)S(1)} %collective-permute-done.24.rest_1_), channel_id=1, source_target_pairs={{0,1},{1,0},{2,3},{3,2},{4,5},{5,4},{6,7},{7,6},{8,9},{9,8},{10,11... | collective-permute-start | bytes 368648 | tf_op jit(solution)/shard_map/ppermute | solution.py:419
  45.6 7.5 %collective-permute-start.25 = (bf16[2,3,80,128]{3,2,1,0:T(8,128)(2,1)S(1)}, bf16[2,3,80,128]{3,2,1,0:T(8,128)(2,1)S(1)}, u32[]{:S(2)}, u32[]{:S(2)}) collective-permute-start(bf16[2,3,80,128]{3,2,1,0:T(8,128)(2,1)S(1)} %collective-permute-done.23.rest_0_), channel_id=1, source_target_pairs={{0,1},{1,0},{2,3},{3,2},{4,5},{5,4},{6,7},{7,6},{8,9},{9,8},{10,11... | collective-permute-start | bytes 368648 | tf_op jit(solution)/shard_map/ppermute | solution.py:419
  46.9 20.3 %collective-permute-start.6 = (bf16[4,3,80,128]{3,2,1,0:T(8,128)(2,1)S(1)}, bf16[4,3,80,128]{3,2,1,0:T(8,128)(2,1)S(1)}, u32[]{:S(2)}, u32[]{:S(2)}) collective-permute-start(bf16[4,3,80,128]{3,2,1,0:T(8,128)(2,1)S(1)} %pad_maximum_fusion.rest_0_), channel_id=1, source_target_pairs={{0,1},{1,0},{2,3},{3,2},{4,5},{5,4},{6,7},{7,6},{8,9},{9,8},{10,11... | collective-permute-start | bytes 737288 | tf_op jit(solution)/shard_map/ppermute | solution.py:419
  47.8 19.9 %collective-permute-start.8 = (bf16[4,3,80,128]{3,2,1,0:T(8,128)(2,1)S(1)}, bf16[4,3,80,128]{3,2,1,0:T(8,128)(2,1)S(1)}, u32[]{:S(2)}, u32[]{:S(2)}) collective-permute-start(bf16[4,3,80,128]{3,2,1,0:T(8,128)(2,1)S(1)} %collective-permute-done.4.rest_2_), channel_id=1, source_target_pairs={{0,1},{1,0},{2,3},{3,2},{4,5},{5,4},{6,7},{7,6},{8,9},{9,8},{10,11... | collective-permute-start | bytes 737288 | tf_op jit(solution)/shard_map/ppermute | solution.py:419
  48.5 20.8 %collective-permute-start.7 = (bf16[4,3,80,128]{3,2,1,0:T(8,128)(2,1)S(1)}, bf16[4,3,80,128]{3,2,1,0:T(8,128)(2,1)S(1)}, u32[]{:S(2)}, u32[]{:S(2)}) collective-permute-start(bf16[4,3,80,128]{3,2,1,0:T(8,128)(2,1)S(1)} %collective-permute-done.3.rest_1_), channel_id=1, source_target_pairs={{0,1},{1,0},{2,3},{3,2},{4,5},{5,4},{6,7},{7,6},{8,9},{9,8},{10,11... | collective-permute-start | bytes 737288 | tf_op jit(solution)/shard_map/ppermute | solution.py:419
  53.0 17.8 %collective-permute-start.9 = (bf16[4,3,80,128]{3,2,1,0:T(8,128)(2,1)S(1)}, bf16[4,3,80,128]{3,2,1,0:T(8,128)(2,1)S(1)}, u32[]{:S(2)}, u32[]{:S(2)}) collective-permute-start(bf16[4,3,80,128]{3,2,1,0:T(8,128)(2,1)S(1)} %collective-permute-done.5.rest_3_), channel_id=1, source_target_pairs={{0,1},{1,0},{2,3},{3,2},{4,5},{5,4},{6,7},{7,6},{8,9},{9,8},{10,11... | collective-permute-start | bytes 737288 | tf_op jit(solution)/shard_map/ppermute | solution.py:419
  53.7 8.4 %collective-permute-start.16 = (bf16[2,3,80,128]{3,2,1,0:T(8,128)(2,1)}, bf16[2,3,80,128]{3,2,1,0:T(8,128)(2,1)}, u32[]{:S(2)}, u32[]{:S(2)}) collective-permute-start(bf16[2,3,80,128]{3,2,1,0:T(8,128)(2,1)} %collective-permute-done.10.rest_2_), channel_id=1, source_target_pairs={{0,1},{1,0},{2,3},{3,2},{4,5},{5,4},{6,7},{7,6},{8,9},{9,8},{10,11... | collective-permute-start | bytes 368648 | tf_op jit(solution)/shard_map/ppermute | solution.py:419
  62.1 10.1 %collective-permute-start.27 = (bf16[256,128]{1,0:T(8,128)(2,1)S(1)}, bf16[256,128]{1,0:T(8,128)(2,1)S(1)}, u32[]{:S(2)}, u32[]{:S(2)}) collective-permute-start(bf16[256,128]{1,0:T(8,128)(2,1)S(1)} %shard_map.94.rest_4_), channel_id=1, source_target_pairs={{0,2},{1,3},{2,0},{3,1},{4,6},{5,7},{6,4},{7,5},{8,10},{9,11},{10,... | collective-permute-start | bytes 196616 | tf_op jit(solution)/shard_map/ppermute | solution.py:419
  67.2 11.1 %collective-permute-start.20 = (bf16[512,128]{1,0:T(8,128)(2,1)S(1)}, bf16[512,128]{1,0:T(8,128)(2,1)S(1)}, u32[]{:S(2)}, u32[]{:S(2)}) collective-permute-start(bf16[512,128]{1,0:T(8,128)(2,1)S(1)} %shard_map.93.rest_0_), channel_id=1, source_target_pairs={{0,2},{1,3},{2,0},{3,1},{4,6},{5,7},{6,4},{7,5},{8,10},{9,11},{10,... | collective-permute-start | bytes 393224 | tf_op jit(solution)/shard_map/ppermute | solution.py:419
  67.7 10.6 %collective-permute-start.21 = (bf16[512,128]{1,0:T(8,128)(2,1)S(1)}, bf16[512,128]{1,0:T(8,128)(2,1)S(1)}, u32[]{:S(2)}, u32[]{:S(2)}) collective-permute-start(bf16[512,128]{1,0:T(8,128)(2,1)S(1)} %shard_map.93.rest_0_), channel_id=1, source_target_pairs={{0,4},{1,5},{2,6},{3,7},{4,0},{5,1},{6,2},{7,3},{8,12},{9,13},{10,... | collective-permute-start | bytes 393224 | tf_op jit(solution)/shard_map/ppermute | solution.py:419
  69.3 9.0 %collective-permute-start.22 = (bf16[512,128]{1,0:T(8,128)(2,1)S(1)}, bf16[512,128]{1,0:T(8,128)(2,1)S(1)}, u32[]{:S(2)}, u32[]{:S(2)}) collective-permute-start(bf16[512,128]{1,0:T(8,128)(2,1)S(1)} %shard_map.93.rest_0_), channel_id=1, source_target_pairs={{0,6},{1,7},{2,4},{3,5},{4,2},{5,3},{6,0},{7,1},{8,14},{9,15},{10,... | collective-permute-start | bytes 393224 | tf_op jit(solution)/shard_map/ppermute | solution.py:419
  70.8 7.5 %collective-permute-start.28 = (bf16[256,128]{1,0:T(8,128)(2,1)S(1)}, bf16[256,128]{1,0:T(8,128)(2,1)S(1)}, u32[]{:S(2)}, u32[]{:S(2)}) collective-permute-start(bf16[256,128]{1,0:T(8,128)(2,1)S(1)} %shard_map.94.rest_4_), channel_id=1, source_target_pairs={{0,4},{1,5},{2,6},{3,7},{4,0},{5,1},{6,2},{7,3},{8,12},{9,13},{10,... | collective-permute-start | bytes 196616 | tf_op jit(solution)/shard_map/ppermute | solution.py:419
  72.2 6.0 %collective-permute-start.29 = (bf16[256,128]{1,0:T(8,128)(2,1)S(1)}, bf16[256,128]{1,0:T(8,128)(2,1)S(1)}, u32[]{:S(2)}, u32[]{:S(2)}) collective-permute-start(bf16[256,128]{1,0:T(8,128)(2,1)S(1)} %shard_map.94.rest_4_), channel_id=1, source_target_pairs={{0,6},{1,7},{2,4},{3,5},{4,2},{5,3},{6,0},{7,1},{8,14},{9,15},{10,... | collective-permute-start | bytes 196616 | tf_op jit(solution)/shard_map/ppermute | solution.py:419
  (23 other events, 197.7 us)
